TPU v7x, 32 devices: a whole 2x2x4 slice. The times are simulated.
32 devices in a mesh: mem: 8 (over z, y), dom: 4 (over x, core).
Axes of the slice: x: 2, y: 2, z: 4, core: 2. Of those that a mesh axis runs over, the one named last changes fastest.
Arguments:
- particle_states: float32 [64, 3, 256, 1024], P('mem', None, 'dom'), may hold values from -6 to 6
- coriolis: float32 [256], replicated, may hold values from -0.6 to 0.6
- observed_cells: int32 [4, 64, 512], P('dom', 'mem'), may hold values from 0 to 1023
- observed_values: float32 [4, 64, 512], P('dom', 'mem'), may hold values from -6 to 15
- resample_draws: int32 [4, 64, 8, 192], P('dom', 'mem'), may hold values from 0 to 63
Outputs:
- analysed: float32 [64, 3, 256, 1024], P('mem', None, 'dom')
All inputs are finite; a program needn't handle non-finite values.
Results may differ from a plain program's by a relative error of at most 0.0003.
Values sent between devices are 32-bit elements; how exact they have to be, the bound alone decides.
No kernel may reach another device: no remote copies, remote signals or barrier semaphores. Data moves between devices by JAX's collectives and lax.ppermute only.
A program may use at most 128 MiB of HBM per device.

v0:
```python
import functools

import jax
import jax.numpy as jnp
from jax import lax
from jax.experimental import pallas as pl
from jax.experimental.pallas import tpu as pltpu
from jax.sharding import PartitionSpec as P


LBLK = 128
LOC = 64
STEPS = 2
SUBLANES = 8
LANES = 128


FLOW_FACTOR = 1.0
PRESSURE_FACTOR = 1.0
OBSERVATION_VARIANCE = 16.0
RELAXATION = 0.5
MERGE_FIRST = 0.75
BLEND_COEF_TWO = (13.0**0.5 + 1.0) / 8.0
MERGE_THIRD = -(13.0**0.5 - 1.0) / 8.0


def edge_rows(array, axis, dim, width):
    count, length = (lax.axis_size(axis), array.shape[dim])
    up = [(i, i + 1) for i in range(count - 1)]
    down = [(j, i) for i, j in up]
    before = lax.ppermute(lax.slice_in_dim(array, length - width, length, axis=dim), axis, up)
    after = lax.ppermute(lax.slice_in_dim(array, 0, width, axis=dim), axis, down)
    return before, after


def forecast_steps(here, there, tiles, final, masked, factor):
    width = here.shape[2]

    def tile(t, shift=0):
        return slice(t * SUBLANES + shift, (t + 1) * SUBLANES + shift)

    def east(quantity):
        return pltpu.roll(quantity, width - 1, 1) - pltpu.roll(quantity, 1, 1)

    def north(ref, field, t):
        return ref[field, tile(t, 1), :] - ref[field, tile(t, -1), :]

    old, new = here, there
    for step in range(STEPS):
        for t in tiles:
            slope = east(old[1, tile(t), :]) + north(old, 2, t)
            new[0, tile(t), :] = masked(
                old[0, tile(t), :] - (0.5 * FLOW_FACTOR) * slope, t
            )
        for t in final if step == STEPS - 1 else tiles:
            turn = factor(t)
            east_old, north_old = old[1, tile(t), :], old[2, tile(t), :]
            east_new = (
                east_old - (0.5 * PRESSURE_FACTOR) * east(new[0, tile(t), :]) + turn * north_old
            )
            north_new = north_old - (0.5 * PRESSURE_FACTOR) * north(new, 0, t) - turn * east_old
            new[1, tile(t), :] = masked(east_new, t)
            new[2, tile(t), :] = masked(north_new, t)
        old, new = new, old
    return old


def coriolis_tile(coriolis_ref, t, width):
    factors = coriolis_ref[t * SUBLANES : (t + 1) * SUBLANES, :]
    return jnp.concatenate([factors] * (width // LANES), axis=1)


def forecast_kernel(count, place_ref, inside_ref, coriolis_ref, states_ref, before_ref, after_ref, *refs):
    rows, width = states_ref.shape[2:]
    margin = before_ref.shape[2]
    outs, (here, there) = refs[:-2], refs[-2:]
    first = 2 * SUBLANES
    last = rows // SUBLANES + 2
    here[:, first - margin : first, :] = before_ref[0]
    here[:, first : first + rows, :] = states_ref[0]
    here[:, first + rows : first + rows + margin, :] = after_ref[0]

    def masked(quantity, t):
        if t == 1:
            return quantity * inside_ref[0]
        if t == last:
            return quantity * inside_ref[1]
        return quantity

    done = forecast_steps(
        here, there, range(1, last + 1), range(2, last), masked,
        lambda t: coriolis_tile(coriolis_ref, t, width),
    )
    if len(outs) == 2:
        outs[0][0] = done[0, first : first + rows, :]
        outs[1][0] = done[1:, first : first + rows, :]
        return
    piece = rows // count
    for d in range(count):
        start = pl.multiple_of(lax.rem(place_ref[0] + d, count) * piece, SUBLANES)
        outs[d][0] = done[0, pl.ds(first + start, piece), :]
        outs[count + d][0] = done[1:, pl.ds(first + start, piece), :]


def coriolis_frame(coriolis, band_index, rows):
    padded = jnp.pad(coriolis, (2 * SUBLANES, 2 * SUBLANES))
    spread = jnp.broadcast_to(padded[:, None], padded.shape + (LANES,))
    return lax.dynamic_slice_in_dim(spread, band_index * rows, rows + 4 * SUBLANES)


def forecast_cost(states, rows):
    size = states.size * rows // states.shape[2]
    return pl.CostEstimate(flops=40 * size * STEPS, bytes_accessed=8 * size, transcendentals=0)


def forecast_pieces(states, before, after, factors, axis, band_index, band_count):
    members, fields, rows, width = states.shape
    count = lax.axis_size(axis)
    margin = before.shape[2]
    piece = rows // count
    whole = piece % SUBLANES != 0
    extents = (rows,) if whole else (piece,) * count
    place = lax.axis_index(axis).astype(jnp.int32).reshape(1)
    inside = jnp.stack([band_index > 0, band_index < band_count - 1]).astype(jnp.float32)
    found = pl.pallas_call(
        functools.partial(forecast_kernel, count),
        grid=(members,),
        in_specs=[
            pl.BlockSpec(memory_space=pltpu.SMEM),
            pl.BlockSpec(memory_space=pltpu.SMEM),
            pl.BlockSpec(factors.shape, lambda m: (0, 0)),
            pl.BlockSpec((1, fields, rows, width), lambda m: (m, 0, 0, 0)),
            pl.BlockSpec((1, fields, margin, width), lambda m: (m, 0, 0, 0)),
            pl.BlockSpec((1, fields, margin, width), lambda m: (m, 0, 0, 0)),
        ],
        out_specs=[pl.BlockSpec((1, r, width), lambda m: (m, 0, 0)) for r in extents]
        + [pl.BlockSpec((1, fields - 1, r, width), lambda m: (m, 0, 0, 0)) for r in extents],
        out_shape=[jax.ShapeDtypeStruct((members, r, width), jnp.float32) for r in extents]
        + [jax.ShapeDtypeStruct((members, fields - 1, r, width), jnp.float32) for r in extents],
        scratch_shapes=[pltpu.VMEM((fields, factors.shape[0], width), jnp.float32)] * 2,
        cost_estimate=forecast_cost(states, rows),
    )(place, inside, factors, states, before, after)
    if whole:
        return row_pieces(found[0], axis, 1), row_pieces(found[1], axis, 2)
    return list(found[:count]), list(found[count:])


def tapering(cells, grid_width, block_cells, length):
    longitude = cells.astype(jnp.float32)
    tile_total = grid_width // block_cells
    centre = jnp.arange(tile_total).astype(jnp.float32) * block_cells + 0.5 * (block_cells - 1)
    distance = jnp.abs(longitude[..., :, None] - centre)
    distance = jnp.minimum(distance, grid_width - distance)
    return jnp.exp(-0.5 * (distance / length) ** 2)


def member_weights(heights, cells, values, block_cells, length):
    grid_width = heights.shape[-1]
    chosen_cells = (
        cells[:, None, :] == lax.broadcasted_iota(jnp.int32, (1, grid_width, 1), 1)
    ).astype(jnp.float32)
    observed = jnp.einsum("erl,rlo->reo", heights, chosen_cells, precision=lax.Precision.HIGHEST)
    misfit = (values[:, None, :] - observed) ** 2
    taper_weights = tapering(cells, grid_width, block_cells, length)
    likelihood = (
        -0.5
        / OBSERVATION_VARIANCE
        * jnp.einsum("reo,rob->rbe", misfit, taper_weights, precision=lax.Precision.HIGHEST)
    )
    largest = jnp.max(likelihood, axis=-1, keepdims=True)
    scaled = jnp.exp(likelihood - largest)
    return scaled / jnp.sum(scaled, axis=-1, keepdims=True)


def mixing_matrix(weights, draws):
    member_count = weights.shape[-1]
    split = draws.reshape(draws.shape[:-1] + (3, member_count))
    column = lax.broadcasted_iota(jnp.int32, (1, 1, 1, member_count), 3)
    picks = MERGE_FIRST * (split[:, :, 0, :, None] == column).astype(jnp.float32)
    picks = picks + BLEND_COEF_TWO * (split[:, :, 1, :, None] == column).astype(jnp.float32)
    picks = picks + MERGE_THIRD * (split[:, :, 2, :, None] == column).astype(jnp.float32)
    return (1.0 - RELAXATION) * weights[:, :, None, :] + RELAXATION * picks


def merge_fields(members, mixing, block_cells):
    member_count, fields, count_of_rows, grid_width = members.shape
    blocks = members.reshape(
        member_count, fields, count_of_rows, grid_width // block_cells, block_cells
    )
    updated = jnp.einsum("rbek,kfrbc->efrbc", mixing, blocks, precision=lax.Precision.HIGHEST)
    return updated.reshape(member_count, fields, count_of_rows, grid_width)


def send_all(pieces, axis):
    count = lax.axis_size(axis)
    received = [pieces[0]]
    for d in range(1, count):
        received.append(lax.ppermute(pieces[d], axis, [(i, (i + d) % count) for i in range(count)]))
    return received


def row_pieces(array, axis, dim):
    count = lax.axis_size(axis)
    own = lax.axis_index(axis)
    length = array.shape[dim] // count
    return [
        lax.dynamic_slice_in_dim(array, lax.rem(own + d, count) * length, length, axis=dim)
        for d in range(count)
    ]


def put_back(whole, received, axis, field):
    count = lax.axis_size(axis)
    own = lax.axis_index(axis)
    length = received[0].shape[2]
    for d, piece in enumerate(received):
        start = lax.rem(own + count - d, count) * length
        whole = lax.dynamic_update_slice(whole, piece, (0, field, start, 0))
    return whole


def relative_draws(draws, axis, members_dev):
    count = lax.axis_size(axis)
    own = lax.axis_index(axis)
    distance = lax.rem(own + count - draws // members_dev, count)
    place = distance * members_dev + draws % members_dev
    split = place.reshape(place.shape[:-1] + (3, count, members_dev))
    doubled = jnp.concatenate([split, split], axis=-2)
    turned = lax.dynamic_slice_in_dim(doubled, own, count, axis=-2)
    return turned.reshape(draws.shape)


def body(particle_states, coriolis, observed_cells, observed_values, resample_draws):
    members_dev, _, count_of_rows, _ = particle_states.shape
    count = lax.axis_size("mem")
    band_index = lax.axis_index("dom")
    factors = coriolis_frame(coriolis, band_index, count_of_rows)
    before, after = edge_rows(particle_states, "dom", 2, 2 * STEPS)
    heights, winds = forecast_pieces(
        particle_states, before, after, factors, "mem", band_index, lax.axis_size("dom")
    )
    heights = send_all(heights, "mem")
    winds_all = send_all(winds, "mem")
    heights = jnp.concatenate(heights, axis=0)
    winds_all = jnp.concatenate(winds_all, axis=0)

    cells = observed_cells[0]
    values = observed_values[0]
    draws = relative_draws(resample_draws[0], "mem", members_dev)
    weights = member_weights(heights, cells, values, LBLK, LOC)
    mixing = mixing_matrix(weights, draws)

    def hand_back(members):
        updated = merge_fields(members, mixing, LBLK)
        pieces = [updated[d * members_dev : (d + 1) * members_dev] for d in range(count)]
        return send_all(pieces, "mem")

    analysed = jnp.zeros(particle_states.shape, particle_states.dtype)
    analysed = put_back(analysed, hand_back(heights[:, None]), "mem", 0)
    return put_back(analysed, hand_back(winds_all), "mem", 1)


def solution(mesh):
    return jax.shard_map(
        body,
        mesh=mesh,
        in_specs=(
            P("mem", None, "dom", None),
            P(),
            P("dom", "mem", None),
            P("dom", "mem", None),
            P("dom", "mem", None, None),
        ),
        out_specs=P("mem", None, "dom", None),
        check_vma=False,
    )
```

profile of v0, /device:TPU:30, one launch (start us, length us, event | category | flops | bytes accessed | tf_op | source)
XLA Modules:
  0.0 318.3 jit_solution(17500517221666337770)
XLA Ops:
  1.6 1.9 collective-permute-start
  3.5 3.6 %collective-permute-start.1 = (f32[8,3,4,1024]{3,2,1,0:T(4,128)S(1)}, f32[8,3,4,1024]{3,2,1,0:T(4,128)S(1)}, u32[]{:S(2)}, u32[]{:S(2)}) collective-permute-start(f32[8,3,4,1024]{3,2,1,0:T(4,128)S(1)} %get-tuple-element.37), channel_id=1, source_target_pairs={{1,0},{2,1},{3,2},{5,4},{6,5},{7,6},{9,8},{10,9},{11,10},{13,12},{... | collective-permute-start | bytes 1179656 | tf_op jit(solution)/shard_map/ppermute | solution.py:32
  13.2 10.5 %shard_map.55 = (f32[8,8,1024]{2,1,0:T(8,128)}, f32[8,8,1024]{2,1,0:T(8,128)}, f32[8,8,1024]{2,1,0:T(8,128)}, f32[8,8,1024]{2,1,0:T(8,128)}, f32[8,8,1024]{2,1,0...) custom-call(s32[1]{0:T(128)} %bitcast.place_ref, ...), custom_call_target="tpu_custom_call" | custom-call | flops 125829120 | bytes 12582912 | tf_op jit(solution)/shard_map/pallas_call | solution.py:125
  31.0 2.2 collective-permute-done.2
  33.7 5.0 %collective-permute-done.3 = f32[8,8,1024]{2,1,0:T(8,128)S(1)} collective-permute-done((f32[8,8,1024]{2,1,0:T(8,128)}, f32[8,8,1024]{2,1,0:T(8,128)S(1)}, u32[]{:S(2)}, u32[]{:S(2)}) %collective-permute-start.3) | collective-permute-done | bytes 262176 | tf_op jit(solution)/shard_map/ppermute | solution.py:198
  38.7 26.0 %collective-permute-done.4 = f32[8,8,1024]{2,1,0:T(8,128)S(1)} collective-permute-done((f32[8,8,1024]{2,1,0:T(8,128)}, f32[8,8,1024]{2,1,0:T(8,128)S(1)}, u32[]{:S(2)}, u32[]{:S(2)}) %collective-permute-start.4) | collective-permute-done | bytes 262176 | tf_op jit(solution)/shard_map/ppermute | solution.py:198
  64.7 9.6 %collective-permute-start.7 = (f32[8,8,1024]{2,1,0:T(8,128)}, f32[8,8,1024]{2,1,0:T(8,128)S(1)}, u32[]{:S(2)}, u32[]{:S(2)}) collective-permute-start(f32[8,8,1024]{2,1,0:T(8,128)} %get-tuple-element.27), channel_id=1, source_target_pairs={{0,24},{4,28},{8,0},{12,4},{16,8},{20,12},{24,16},{28,20},{1,25},{... | collective-permute-start | bytes 786440 | tf_op jit(solution)/shard_map/ppermute | solution.py:198
  74.4 36.3 %collective-permute-done.5 = f32[8,8,1024]{2,1,0:T(8,128)S(1)} collective-permute-done((f32[8,8,1024]{2,1,0:T(8,128)}, f32[8,8,1024]{2,1,0:T(8,128)S(1)}, u32[]{:S(2)}, u32[]{:S(2)}) %collective-permute-start.5) | collective-permute-done | bytes 262176 | tf_op jit(solution)/shard_map/ppermute | solution.py:198
  111.0 9.1 %collective-permute-done.8 = f32[8,8,1024]{2,1,0:T(8,128)S(1)} collective-permute-done((f32[8,8,1024]{2,1,0:T(8,128)}, f32[8,8,1024]{2,1,0:T(8,128)S(1)}, u32[]{:S(2)}, u32[]{:S(2)}) %collective-permute-start.8) | collective-permute-done | bytes 262176 | tf_op jit(solution)/shard_map/ppermute | solution.py:198
  120.1 10.5 %collective-permute-start.20 = (f32[8,2,8,1024]{3,2,1,0:T(8,128)S(1)}, f32[8,2,8,1024]{3,2,1,0:T(8,128)S(1)}, u32[]{:S(2)}, u32[]{:S(2)}) collective-permute-start(f32[8,2,8,1024]{3,2,1,0:T(8,128)S(1)} %copy-done.7), channel_id=1, source_target_pairs={{0,20},{4,24},{8,28},{12,0},{16,4},{20,8},{24,12},{28,16},{1,21},{... | collective-permute-start | bytes 1572872 | tf_op jit(solution)/shard_map/ppermute | solution.py:198
  130.6 6.8 %fusion.18 = f32[8,64,512]{2,1,0:T(8,128)S(1)} fusion(s32[8,512]{1,0:T(8,128)S(1)} %bitcast.62, f32[64,8,1024]{2,1,0:T(8,128)S(1)} %constant_dynamic-update-slice_fusion, f32[8,512]{1,0:T(8,128)S(1)} %bitcast.63), kind=kOutput, calls=%fused_computation.19 | convolution fusion | flops 3225944064 | bytes 3178496 | tf_op jit(solution)/shard_map/erl,rlo->reo/dot_general | solution.py:162
  139.9 6.8 %fusion.12 = f32[64,1,8,8,128]{4,0,3,2,1:T(8,128)S(1)} fusion(f32[64,8,8,128]{3,1,2,0:T(8,128)S(1)} %bitcast.61, s32[8,8,64]{2,1,0:T(8,128)S(1)} %get-tuple-element.56, s32[8,8,64]{2,1,0:T(8,128)S(1)} %get-tuple-element.57, s32[8,8,64]{2,1,0:T(8,128)S(1)} %get-tuple-element.55, f32[8,8,64]{2,1,0:T(8,128)S(1)} %divide_multiply_fusion), kind=kOutput, calls=%fused_computation.15 | convolution fusion | flops 405274624 | bytes 4259840 | tf_op jit(solution)/shard_map/rbek,kfrbc->efrbc/dot_general | solution.py:190
  147.0 3.5 %broadcast_in_dim.4 = f32[8,3,64,1024]{3,2,1,0:T(8,128)} broadcast(f32[]{:T(128)} %constant.92.clone.1), dimensions={} | broadcast | bytes 6291460 | tf_op jit(solution)/shard_map/broadcast_in_dim | solution.py:258
  155.2 3.3 %collective-permute-start.22 = (f32[8,2,8,1024]{3,2,1,0:T(8,128)S(1)}, f32[8,2,8,1024]{3,2,1,0:T(8,128)S(1)}, u32[]{:S(2)}, u32[]{:S(2)}) collective-permute-start(f32[8,2,8,1024]{3,2,1,0:T(8,128)S(1)} %copy-done.5), channel_id=1, source_target_pairs={{0,28},{4,0},{8,4},{12,8},{16,12},{20,16},{24,20},{28,24},{1,29},{... | collective-permute-start | bytes 1572872 | tf_op jit(solution)/shard_map/ppermute | solution.py:198
  158.6 3.3 %collective-permute-start.9 = (f32[8,1,8,1024]{3,1,2,0:T(1,128)S(1)}, f32[8,1,8,1024]{3,1,2,0:T(1,128)S(1)}, u32[]{:S(2)}, u32[]{:S(2)}) collective-permute-start(f32[8,1,8,1024]{3,1,2,0:T(1,128)S(1)} %bitcast.59), channel_id=1, source_target_pairs={{0,4},{4,8},{8,12},{12,16},{16,20},{20,24},{24,28},{28,0},{1,5},{5... | collective-permute-start | bytes 786440 | tf_op jit(solution)/shard_map/ppermute | solution.py:198
  162.6 18.9 %collective-permute-done.20 = f32[8,2,8,1024]{3,2,1,0:T(8,128)S(1)} collective-permute-done((f32[8,2,8,1024]{3,2,1,0:T(8,128)S(1)}, f32[8,2,8,1024]{3,2,1,0:T(8,128)S(1)}, u32[]{:S(2)}, u32[]{:S(2)}) %collective-permute-start.20) | collective-permute-done | bytes 524320 | tf_op jit(solution)/shard_map/ppermute | solution.py:198
  181.8 17.4 %collective-permute-start.13 = (f32[8,1,8,1024]{3,1,2,0:T(1,128)}, f32[8,1,8,1024]{3,1,2,0:T(1,128)S(1)}, u32[]{:S(2)}, u32[]{:S(2)}) collective-permute-start(f32[8,1,8,1024]{3,1,2,0:T(1,128)} %bitcast.17), channel_id=1, source_target_pairs={{0,20},{4,24},{8,28},{12,0},{16,4},{20,8},{24,12},{28,16},{1,21},{... | collective-permute-start | bytes 786440 | tf_op jit(solution)/shard_map/ppermute | solution.py:198
  199.2 9.1 %fusion.5 = f32[64,2,8,8,128]{4,0,1,3,2:T(8,128)S(1)} fusion(f32[64,2,8,8,128]{4,2,3,1,0:T(8,128)S(1)} %bitcast.60, s32[8,8,64]{2,1,0:T(8,128)S(1)} %get-tuple-element.56, s32[8,8,64]{2,1,0:T(8,128)S(1)} %get-tuple-element.57, s32[8,8,64]{2,1,0:T(8,128)S(1)} %get-tuple-element.55, f32[8,8,64]{2,1,0:T(8,128)S(1)} %divide_multiply_fusion), kind=kOutput, calls=%fused_computation.6 | convolution fusion | flops 807927808 | bytes 8454144 | tf_op jit(solution)/shard_map/rbek,kfrbc->efrbc/dot_general | solution.py:190
  210.5 3.4 %collective-permute-start.15 = (f32[8,1,8,1024]{3,1,2,0:T(1,128)}, f32[8,1,8,1024]{3,1,2,0:T(1,128)}, u32[]{:S(2)}, u32[]{:S(2)}) collective-permute-start(f32[8,1,8,1024]{3,1,2,0:T(1,128)} %bitcast.19), channel_id=1, source_target_pairs={{0,28},{4,0},{8,4},{12,8},{16,12},{20,16},{24,20},{28,24},{1,29},{... | collective-permute-start | bytes 786440 | tf_op jit(solution)/shard_map/ppermute | solution.py:198
  215.6 1.9 slice.133
  217.5 2.0 copy.31
  219.5 1.9 slice.135
  221.4 3.3 %collective-permute-start.23 = (f32[8,2,8,1024]{3,2,1,0:T(8,128)}, f32[8,2,8,1024]{3,2,1,0:T(8,128)}, u32[]{:S(2)}, u32[]{:S(2)}) collective-permute-start(f32[8,2,8,1024]{3,2,1,0:T(8,128)} %slice.135), channel_id=1, source_target_pairs={{0,4},{4,8},{8,12},{12,16},{16,20},{20,24},{24,28},{28,0},{1,5},{5... | collective-permute-start | bytes 1572872 | tf_op jit(solution)/shard_map/ppermute | solution.py:198
  227.4 1.9 slice.137
  232.5 1.9 slice.139
  236.3 6.4 %collective-permute-start.26 = (f32[8,2,8,1024]{3,2,1,0:T(8,128)}, f32[8,2,8,1024]{3,2,1,0:T(8,128)}, u32[]{:S(2)}, u32[]{:S(2)}) collective-permute-start(f32[8,2,8,1024]{3,2,1,0:T(8,128)} %slice.141), channel_id=1, source_target_pairs={{0,16},{4,20},{8,24},{12,28},{16,0},{20,4},{24,8},{28,12},{1,17},{... | collective-permute-start | bytes 1572872 | tf_op jit(solution)/shard_map/ppermute | solution.py:198
  244.6 6.9 %collective-permute-start.27 = (f32[8,2,8,1024]{3,2,1,0:T(8,128)S(1)}, f32[8,2,8,1024]{3,2,1,0:T(8,128)}, u32[]{:S(2)}, u32[]{:S(2)}) collective-permute-start(f32[8,2,8,1024]{3,2,1,0:T(8,128)S(1)} %slice.143), channel_id=1, source_target_pairs={{0,20},{4,24},{8,28},{12,0},{16,4},{20,8},{24,12},{28,16},{1,21},{... | collective-permute-start | bytes 1572872 | tf_op jit(solution)/shard_map/ppermute | solution.py:198
  254.6 1.9 constant_dynamic-update-slice_fusion.22
  256.5 25.9 %collective-permute-start.29 = (f32[8,2,8,1024]{3,2,1,0:T(8,128)S(1)}, f32[8,2,8,1024]{3,2,1,0:T(8,128)S(1)}, u32[]{:S(2)}, u32[]{:S(2)}) collective-permute-start(f32[8,2,8,1024]{3,2,1,0:T(8,128)S(1)} %slice.147), channel_id=1, source_target_pairs={{0,28},{4,0},{8,4},{12,8},{16,12},{20,16},{24,20},{28,24},{1,29},{... | collective-permute-start | bytes 1572872 | tf_op jit(solution)/shard_map/ppermute | solution.py:198
  284.3 1.9 constant_dynamic-update-slice_fusion.20
  286.2 14.7 %collective-permute-done.26 = f32[8,2,8,1024]{3,2,1,0:T(8,128)} collective-permute-done((f32[8,2,8,1024]{3,2,1,0:T(8,128)}, f32[8,2,8,1024]{3,2,1,0:T(8,128)}, u32[]{:S(2)}, u32[]{:S(2)}) %collective-permute-start.26) | collective-permute-done | bytes 524320 | tf_op jit(solution)/shard_map/ppermute | solution.py:198
  302.9 11.9 %collective-permute-done.27 = f32[8,2,8,1024]{3,2,1,0:T(8,128)} collective-permute-done((f32[8,2,8,1024]{3,2,1,0:T(8,128)S(1)}, f32[8,2,8,1024]{3,2,1,0:T(8,128)}, u32[]{:S(2)}, u32[]{:S(2)}) %collective-permute-start.27) | collective-permute-done | bytes 524320 | tf_op jit(solution)/shard_map/ppermute | solution.py:198
  (125 shorter events, 47.9 us)
Async XLA Ops:
  1.6 9.7 %collective-permute-start = (f32[8,3,4,1024]{3,2,1,0:T(4,128)S(1)}, f32[8,3,4,1024]{3,2,1,0:T(4,128)S(1)}, u32[]{:S(2)}, u32[]{:S(2)}) collective-permute-start(f32[8,3,4,1024]{3,2,1,0:T(4,128)S(1)} %get-tuple-element.38), channel_id=1, source_target_pairs={{0,1},{1,2},{2,3},{4,5},{5,6},{6,7},{8,9},{9,10},{10,11},{12,13},{... | collective-permute-start | bytes 1179656 | tf_op jit(solution)/shard_map/ppermute | solution.py:31
  3.5 8.9 %collective-permute-start.1 = (f32[8,3,4,1024]{3,2,1,0:T(4,128)S(1)}, f32[8,3,4,1024]{3,2,1,0:T(4,128)S(1)}, u32[]{:S(2)}, u32[]{:S(2)}) collective-permute-start(f32[8,3,4,1024]{3,2,1,0:T(4,128)S(1)} %get-tuple-element.37), channel_id=1, source_target_pairs={{1,0},{2,1},{3,2},{5,4},{6,5},{7,6},{9,8},{10,9},{11,10},{13,12},{... | collective-permute-start | bytes 1179656 | tf_op jit(solution)/shard_map/ppermute | solution.py:32
  23.7 106.9 %copy-start.3 = (s32[1,8,512]{2,1,0:T(8,128)S(1)}, s32[1,8,512]{2,1,0:T(8,128)}, u32[]{:S(2)}) copy-start(s32[1,8,512]{2,1,0:T(8,128)} %param.7) | copy-start | bytes 49156
  23.7 106.9 %copy-start.9 = (f32[1,8,512]{2,1,0:T(8,128)S(1)}, f32[1,8,512]{2,1,0:T(8,128)}, u32[]{:S(2)}) copy-start(f32[1,8,512]{2,1,0:T(8,128)} %param.8) | copy-start | bytes 49156
  23.7 9.4 %collective-permute-start.2 = (f32[8,8,1024]{2,1,0:T(8,128)}, f32[8,8,1024]{2,1,0:T(8,128)S(1)}, u32[]{:S(2)}, u32[]{:S(2)}) collective-permute-start(f32[8,8,1024]{2,1,0:T(8,128)} %get-tuple-element.22), channel_id=1, source_target_pairs={{0,4},{4,8},{8,12},{12,16},{16,20},{20,24},{24,28},{28,0},{1,5},{5... | collective-permute-start | bytes 786440 | tf_op jit(solution)/shard_map/ppermute | solution.py:198
  23.9 14.8 %collective-permute-start.3 = (f32[8,8,1024]{2,1,0:T(8,128)}, f32[8,8,1024]{2,1,0:T(8,128)S(1)}, u32[]{:S(2)}, u32[]{:S(2)}) collective-permute-start(f32[8,8,1024]{2,1,0:T(8,128)} %get-tuple-element.23), channel_id=1, source_target_pairs={{0,8},{4,12},{8,16},{12,20},{16,24},{20,28},{24,0},{28,4},{1,9},{5... | collective-permute-start | bytes 786440 | tf_op jit(solution)/shard_map/ppermute | solution.py:198
  26.6 128.5 %collective-permute-start.16 = (f32[8,2,8,1024]{3,2,1,0:T(8,128)}, f32[8,2,8,1024]{3,2,1,0:T(8,128)S(1)}, u32[]{:S(2)}, u32[]{:S(2)}) collective-permute-start(f32[8,2,8,1024]{3,2,1,0:T(8,128)} %get-tuple-element.30), channel_id=1, source_target_pairs={{0,4},{4,8},{8,12},{12,16},{16,20},{20,24},{24,28},{28,0},{1,5},{5... | collective-permute-start | bytes 1572872 | tf_op jit(solution)/shard_map/ppermute | solution.py:198
  28.2 127.0 %collective-permute-start.17 = (f32[8,2,8,1024]{3,2,1,0:T(8,128)}, f32[8,2,8,1024]{3,2,1,0:T(8,128)S(1)}, u32[]{:S(2)}, u32[]{:S(2)}) collective-permute-start(f32[8,2,8,1024]{3,2,1,0:T(8,128)} %get-tuple-element.31), channel_id=1, source_target_pairs={{0,8},{4,12},{8,16},{12,20},{16,24},{20,28},{24,0},{28,4},{1,9},{5... | collective-permute-start | bytes 1572872 | tf_op jit(solution)/shard_map/ppermute | solution.py:198
  29.7 35.0 %collective-permute-start.4 = (f32[8,8,1024]{2,1,0:T(8,128)}, f32[8,8,1024]{2,1,0:T(8,128)S(1)}, u32[]{:S(2)}, u32[]{:S(2)}) collective-permute-start(f32[8,8,1024]{2,1,0:T(8,128)} %get-tuple-element.24), channel_id=1, source_target_pairs={{0,12},{4,16},{8,20},{12,24},{16,28},{20,0},{24,4},{28,8},{1,13},{... | collective-permute-start | bytes 786440 | tf_op jit(solution)/shard_map/ppermute | solution.py:198
  33.2 77.6 %collective-permute-start.5 = (f32[8,8,1024]{2,1,0:T(8,128)}, f32[8,8,1024]{2,1,0:T(8,128)S(1)}, u32[]{:S(2)}, u32[]{:S(2)}) collective-permute-start(f32[8,8,1024]{2,1,0:T(8,128)} %get-tuple-element.25), channel_id=1, source_target_pairs={{0,16},{4,20},{8,24},{12,28},{16,0},{20,4},{24,8},{28,12},{1,17},{... | collective-permute-start | bytes 786440 | tf_op jit(solution)/shard_map/ppermute | solution.py:198
  38.7 72.0 %collective-permute-start.6 = (f32[8,8,1024]{2,1,0:T(8,128)}, f32[8,8,1024]{2,1,0:T(8,128)S(1)}, u32[]{:S(2)}, u32[]{:S(2)}) collective-permute-start(f32[8,8,1024]{2,1,0:T(8,128)} %get-tuple-element.26), channel_id=1, source_target_pairs={{0,20},{4,24},{8,28},{12,0},{16,4},{20,8},{24,12},{28,16},{1,21},{... | collective-permute-start | bytes 786440 | tf_op jit(solution)/shard_map/ppermute | solution.py:198
  64.7 46.1 %collective-permute-start.7 = (f32[8,8,1024]{2,1,0:T(8,128)}, f32[8,8,1024]{2,1,0:T(8,128)S(1)}, u32[]{:S(2)}, u32[]{:S(2)}) collective-permute-start(f32[8,8,1024]{2,1,0:T(8,128)} %get-tuple-element.27), channel_id=1, source_target_pairs={{0,24},{4,28},{8,0},{12,4},{16,8},{20,12},{24,16},{28,20},{1,25},{... | collective-permute-start | bytes 786440 | tf_op jit(solution)/shard_map/ppermute | solution.py:198
  110.7 9.4 %collective-permute-start.8 = (f32[8,8,1024]{2,1,0:T(8,128)}, f32[8,8,1024]{2,1,0:T(8,128)S(1)}, u32[]{:S(2)}, u32[]{:S(2)}) collective-permute-start(f32[8,8,1024]{2,1,0:T(8,128)} %get-tuple-element.28), channel_id=1, source_target_pairs={{0,28},{4,0},{8,4},{12,8},{16,12},{20,16},{24,20},{28,24},{1,29},{... | collective-permute-start | bytes 786440 | tf_op jit(solution)/shard_map/ppermute | solution.py:198
  110.8 47.8 %collective-permute-start.18 = (f32[8,2,8,1024]{3,2,1,0:T(8,128)}, f32[8,2,8,1024]{3,2,1,0:T(8,128)S(1)}, u32[]{:S(2)}, u32[]{:S(2)}) collective-permute-start(f32[8,2,8,1024]{3,2,1,0:T(8,128)} %get-tuple-element.32), channel_id=1, source_target_pairs={{0,12},{4,16},{8,20},{12,24},{16,28},{20,0},{24,4},{28,8},{1,13},{... | collective-permute-start | bytes 1572872 | tf_op jit(solution)/shard_map/ppermute | solution.py:198
  110.9 51.1 %collective-permute-start.19 = (f32[8,2,8,1024]{3,2,1,0:T(8,128)S(1)}, f32[8,2,8,1024]{3,2,1,0:T(8,128)S(1)}, u32[]{:S(2)}, u32[]{:S(2)}) collective-permute-start(f32[8,2,8,1024]{3,2,1,0:T(8,128)S(1)} %copy-done.8), channel_id=1, source_target_pairs={{0,16},{4,20},{8,24},{12,28},{16,0},{20,4},{24,8},{28,12},{1,17},{... | collective-permute-start | bytes 1572872 | tf_op jit(solution)/shard_map/ppermute | solution.py:198
  120.1 61.5 %collective-permute-start.20 = (f32[8,2,8,1024]{3,2,1,0:T(8,128)S(1)}, f32[8,2,8,1024]{3,2,1,0:T(8,128)S(1)}, u32[]{:S(2)}, u32[]{:S(2)}) collective-permute-start(f32[8,2,8,1024]{3,2,1,0:T(8,128)S(1)} %copy-done.7), channel_id=1, source_target_pairs={{0,20},{4,24},{8,28},{12,0},{16,4},{20,8},{24,12},{28,16},{1,21},{... | collective-permute-start | bytes 1572872 | tf_op jit(solution)/shard_map/ppermute | solution.py:198
  155.1 26.5 %collective-permute-start.21 = (f32[8,2,8,1024]{3,2,1,0:T(8,128)S(1)}, f32[8,2,8,1024]{3,2,1,0:T(8,128)S(1)}, u32[]{:S(2)}, u32[]{:S(2)}) collective-permute-start(f32[8,2,8,1024]{3,2,1,0:T(8,128)S(1)} %copy-done.6), channel_id=1, source_target_pairs={{0,24},{4,28},{8,0},{12,4},{16,8},{20,12},{24,16},{28,20},{1,25},{... | collective-permute-start | bytes 1572872 | tf_op jit(solution)/shard_map/ppermute | solution.py:198
  155.2 26.5 %collective-permute-start.22 = (f32[8,2,8,1024]{3,2,1,0:T(8,128)S(1)}, f32[8,2,8,1024]{3,2,1,0:T(8,128)S(1)}, u32[]{:S(2)}, u32[]{:S(2)}) collective-permute-start(f32[8,2,8,1024]{3,2,1,0:T(8,128)S(1)} %copy-done.5), channel_id=1, source_target_pairs={{0,28},{4,0},{8,4},{12,8},{16,12},{20,16},{24,20},{28,24},{1,29},{... | collective-permute-start | bytes 1572872 | tf_op jit(solution)/shard_map/ppermute | solution.py:198
  158.6 51.1 %collective-permute-start.9 = (f32[8,1,8,1024]{3,1,2,0:T(1,128)S(1)}, f32[8,1,8,1024]{3,1,2,0:T(1,128)S(1)}, u32[]{:S(2)}, u32[]{:S(2)}) collective-permute-start(f32[8,1,8,1024]{3,1,2,0:T(1,128)S(1)} %bitcast.59), channel_id=1, source_target_pairs={{0,4},{4,8},{8,12},{12,16},{16,20},{20,24},{24,28},{28,0},{1,5},{5... | collective-permute-start | bytes 786440 | tf_op jit(solution)/shard_map/ppermute | solution.py:198
  162.0 48.5 %collective-permute-start.10 = (f32[8,1,8,1024]{3,1,2,0:T(1,128)S(1)}, f32[8,1,8,1024]{3,1,2,0:T(1,128)S(1)}, u32[]{:S(2)}, u32[]{:S(2)}) collective-permute-start(f32[8,1,8,1024]{3,1,2,0:T(1,128)S(1)} %bitcast.58), channel_id=1, source_target_pairs={{0,8},{4,12},{8,16},{12,20},{16,24},{20,28},{24,0},{28,4},{1,9},{5... | collective-permute-start | bytes 786440 | tf_op jit(solution)/shard_map/ppermute | solution.py:198
  181.6 39.9 %collective-permute-start.11 = (f32[8,1,8,1024]{3,1,2,0:T(1,128)}, f32[8,1,8,1024]{3,1,2,0:T(1,128)}, u32[]{:S(2)}, u32[]{:S(2)}) collective-permute-start(f32[8,1,8,1024]{3,1,2,0:T(1,128)} %bitcast.15), channel_id=1, source_target_pairs={{0,12},{4,16},{8,20},{12,24},{16,28},{20,0},{24,4},{28,8},{1,13},{... | collective-permute-start | bytes 786440 | tf_op jit(solution)/shard_map/ppermute | solution.py:198
  181.6 47.7 %collective-permute-start.12 = (f32[8,1,8,1024]{3,1,2,0:T(1,128)}, f32[8,1,8,1024]{3,1,2,0:T(1,128)}, u32[]{:S(2)}, u32[]{:S(2)}) collective-permute-start(f32[8,1,8,1024]{3,1,2,0:T(1,128)} %bitcast.16), channel_id=1, source_target_pairs={{0,16},{4,20},{8,24},{12,28},{16,0},{20,4},{24,8},{28,12},{1,17},{... | collective-permute-start | bytes 786440 | tf_op jit(solution)/shard_map/ppermute | solution.py:198
  181.8 52.7 %collective-permute-start.13 = (f32[8,1,8,1024]{3,1,2,0:T(1,128)}, f32[8,1,8,1024]{3,1,2,0:T(1,128)S(1)}, u32[]{:S(2)}, u32[]{:S(2)}) collective-permute-start(f32[8,1,8,1024]{3,1,2,0:T(1,128)} %bitcast.17), channel_id=1, source_target_pairs={{0,20},{4,24},{8,28},{12,0},{16,4},{20,8},{24,12},{28,16},{1,21},{... | collective-permute-start | bytes 786440 | tf_op jit(solution)/shard_map/ppermute | solution.py:198
  209.7 26.6 %collective-permute-start.14 = (f32[8,1,8,1024]{3,1,2,0:T(1,128)}, f32[8,1,8,1024]{3,1,2,0:T(1,128)}, u32[]{:S(2)}, u32[]{:S(2)}) collective-permute-start(f32[8,1,8,1024]{3,1,2,0:T(1,128)} %bitcast.18), channel_id=1, source_target_pairs={{0,24},{4,28},{8,0},{12,4},{16,8},{20,12},{24,16},{28,20},{1,25},{... | collective-permute-start | bytes 786440 | tf_op jit(solution)/shard_map/ppermute | solution.py:198
  210.5 34.1 %collective-permute-start.15 = (f32[8,1,8,1024]{3,1,2,0:T(1,128)}, f32[8,1,8,1024]{3,1,2,0:T(1,128)}, u32[]{:S(2)}, u32[]{:S(2)}) collective-permute-start(f32[8,1,8,1024]{3,1,2,0:T(1,128)} %bitcast.19), channel_id=1, source_target_pairs={{0,28},{4,0},{8,4},{12,8},{16,12},{20,16},{24,20},{28,24},{1,29},{... | collective-permute-start | bytes 786440 | tf_op jit(solution)/shard_map/ppermute | solution.py:198
  221.4 33.1 %collective-permute-start.23 = (f32[8,2,8,1024]{3,2,1,0:T(8,128)}, f32[8,2,8,1024]{3,2,1,0:T(8,128)}, u32[]{:S(2)}, u32[]{:S(2)}) collective-permute-start(f32[8,2,8,1024]{3,2,1,0:T(8,128)} %slice.135), channel_id=1, source_target_pairs={{0,4},{4,8},{8,12},{12,16},{16,20},{20,24},{24,28},{28,0},{1,5},{5... | collective-permute-start | bytes 1572872 | tf_op jit(solution)/shard_map/ppermute | solution.py:198
  229.3 27.2 %collective-permute-start.24 = (f32[8,2,8,1024]{3,2,1,0:T(8,128)}, f32[8,2,8,1024]{3,2,1,0:T(8,128)}, u32[]{:S(2)}, u32[]{:S(2)}) collective-permute-start(f32[8,2,8,1024]{3,2,1,0:T(8,128)} %slice.137), channel_id=1, source_target_pairs={{0,8},{4,12},{8,16},{12,20},{16,24},{20,28},{24,0},{28,4},{1,9},{5... | collective-permute-start | bytes 1572872 | tf_op jit(solution)/shard_map/ppermute | solution.py:198
  234.5 49.9 %collective-permute-start.25 = (f32[8,2,8,1024]{3,2,1,0:T(8,128)}, f32[8,2,8,1024]{3,2,1,0:T(8,128)}, u32[]{:S(2)}, u32[]{:S(2)}) collective-permute-start(f32[8,2,8,1024]{3,2,1,0:T(8,128)} %slice.139), channel_id=1, source_target_pairs={{0,12},{4,16},{8,20},{12,24},{16,28},{20,0},{24,4},{28,8},{1,13},{... | collective-permute-start | bytes 1572872 | tf_op jit(solution)/shard_map/ppermute | solution.py:198
  236.3 64.7 %collective-permute-start.26 = (f32[8,2,8,1024]{3,2,1,0:T(8,128)}, f32[8,2,8,1024]{3,2,1,0:T(8,128)}, u32[]{:S(2)}, u32[]{:S(2)}) collective-permute-start(f32[8,2,8,1024]{3,2,1,0:T(8,128)} %slice.141), channel_id=1, source_target_pairs={{0,16},{4,20},{8,24},{12,28},{16,0},{20,4},{24,8},{28,12},{1,17},{... | collective-permute-start | bytes 1572872 | tf_op jit(solution)/shard_map/ppermute | solution.py:198
  244.6 70.1 %collective-permute-start.27 = (f32[8,2,8,1024]{3,2,1,0:T(8,128)S(1)}, f32[8,2,8,1024]{3,2,1,0:T(8,128)}, u32[]{:S(2)}, u32[]{:S(2)}) collective-permute-start(f32[8,2,8,1024]{3,2,1,0:T(8,128)S(1)} %slice.143), channel_id=1, source_target_pairs={{0,20},{4,24},{8,28},{12,0},{16,4},{20,8},{24,12},{28,16},{1,21},{... | collective-permute-start | bytes 1572872 | tf_op jit(solution)/shard_map/ppermute | solution.py:198
  254.6 62.1 %collective-permute-start.28 = (f32[8,2,8,1024]{3,2,1,0:T(8,128)S(1)}, f32[8,2,8,1024]{3,2,1,0:T(8,128)S(1)}, u32[]{:S(2)}, u32[]{:S(2)}) collective-permute-start(f32[8,2,8,1024]{3,2,1,0:T(8,128)S(1)} %slice.145), channel_id=1, source_target_pairs={{0,24},{4,28},{8,0},{12,4},{16,8},{20,12},{24,16},{28,20},{1,25},{... | collective-permute-start | bytes 1572872 | tf_op jit(solution)/shard_map/ppermute | solution.py:198
  256.5 61.0 %collective-permute-start.29 = (f32[8,2,8,1024]{3,2,1,0:T(8,128)S(1)}, f32[8,2,8,1024]{3,2,1,0:T(8,128)S(1)}, u32[]{:S(2)}, u32[]{:S(2)}) collective-permute-start(f32[8,2,8,1024]{3,2,1,0:T(8,128)S(1)} %slice.147), channel_id=1, source_target_pairs={{0,28},{4,0},{8,4},{12,8},{16,12},{20,16},{24,20},{28,24},{1,29},{... | collective-permute-start | bytes 1572872 | tf_op jit(solution)/shard_map/ppermute | solution.py:198
  (8 other events, 233.1 us)
where the time goes:
time: 319 us; the launch traced here: 318 us
  waiting for transfers between devices  125 us (39%)
  starting transfers between devices  103 us (32%)
  local copies, waits for them, and re-layouts  51.5 us (16%)
  matrix products  23.7 us (7%)
  Pallas kernels  10.5 us (3%)
  other arithmetic  3.98 us (1%)
    ppermute x28, waiting for transfers between devices, send_all(): lax.ppermute(pieces[d], axis, [(i, (i + d) % count) for i in range(count)])  124 us
    ppermute x28, starting transfers between devices, send_all(): lax.ppermute(pieces[d], axis, [(i, (i + d) % count) for i in range(count)])  97.2 us
    dynamic_update_slice x16, local copies, waits for them, and re-layouts, put_back(): whole = lax.dynamic_update_slice(whole, piece, (0, field, start, 0))  21.7 us
    slice x26, local copies, waits for them, and re-layouts, hand_back(): updated[d * members_dev:(d + 1) * members_dev]  20 us
    dot_general x2, matrix products, merge_fields(): jnp.einsum('rbek,kfrbc->efrbc', mixing, blocks, precision=lax.Precision.H...  15.9 us
    pallas_call x1, Pallas kernels, forecast_pieces(): pl.pallas_call(functools.partial(forecast_kernel, count), grid=(members,)...  10.5 us
    dot_general x1, matrix products, member_weights(): jnp.einsum('erl,rlo->reo', heights, chosen_cells, precision=lax.Precision...  6.8 us
  transfers between devices with their start and end apart: 30, of which 9 were waited for; matrix products, arithmetic and copies ran while one was open for 24% of the time, Pallas kernels for 0%

commit v1 on v0

--- a/solution.py
+++ b/solution.py
@@ -191,12 +191,16 @@
     return updated.reshape(member_count, fields, count_of_rows, grid_width)
 
 
+def by_reach(count):
+    return sorted(range(1, count), key=lambda d: abs(2 * d - count))
+
+
 def send_all(pieces, axis):
     count = lax.axis_size(axis)
-    received = [pieces[0]]
-    for d in range(1, count):
-        received.append(lax.ppermute(pieces[d], axis, [(i, (i + d) % count) for i in range(count)]))
-    return received
+    received = {0: pieces[0]}
+    for d in by_reach(count):
+        received[d] = lax.ppermute(pieces[d], axis, [(i, (i + d) % count) for i in range(count)])
+    return [received[d] for d in range(count)]
 
 
 def row_pieces(array, axis, dim):
@@ -213,7 +217,8 @@
     count = lax.axis_size(axis)
     own = lax.axis_index(axis)
     length = received[0].shape[2]
-    for d, piece in enumerate(received):
+    for d in [0] + by_reach(count)[::-1]:
+        piece = received[d]
         start = lax.rem(own + count - d, count) * length
         whole = lax.dynamic_update_slice(whole, piece, (0, field, start, 0))
     return whole

time: 319 us -> 324 us (1.016)
  the two profiles are of different devices: /device:TPU:30 before, /device:TPU:0 now
where the time goes in v1:
time: 324 us; the launch traced here: 319 us
  starting transfers between devices  128 us (40%)
  waiting for transfers between devices  101 us (31%)
  local copies, waits for them, and re-layouts  51.6 us (16%)
  matrix products  23.7 us (7%)
  Pallas kernels  10.5 us (3%)
  other arithmetic  3.98 us (1%)
    ppermute x28, starting transfers between devices, send_all(): lax.ppermute(pieces[d], axis, [(i, (i + d) % count) for i in range(count)])  124 us
    ppermute x28, waiting for transfers between devices, send_all(): lax.ppermute(pieces[d], axis, [(i, (i + d) % count) for i in range(count)])  101 us
    dynamic_update_slice x16, local copies, waits for them, and re-layouts, put_back(): whole = lax.dynamic_update_slice(whole, piece, (0, field, start, 0))  21.8 us
    slice x26, local copies, waits for them, and re-layouts, hand_back(): updated[d * members_dev:(d + 1) * members_dev]  20 us
    dot_general x2, matrix products, merge_fields(): jnp.einsum('rbek,kfrbc->efrbc', mixing, blocks, precision=lax.Precision.H...  15.9 us
    pallas_call x1, Pallas kernels, forecast_pieces(): pl.pallas_call(functools.partial(forecast_kernel, count), grid=(members,)...  10.5 us
    dot_general x1, matrix products, member_weights(): jnp.einsum('erl,rlo->reo', heights, chosen_cells, precision=lax.Precision...  6.8 us
  transfers between devices with their start and end apart: 30, of which 7 were waited for; matrix products, arithmetic and copies ran while one was open for 24% of the time, Pallas kernels for 0%

profile of v1, /device:TPU:0, one launch (start us, length us, event | category | flops | bytes accessed | tf_op | source)
XLA Modules:
  0.0 319.3 jit_solution(16722567765660762453)
XLA Ops:
  1.6 2.4 collective-permute-start
  10.5 10.5 %shard_map.55 = (f32[8,8,1024]{2,1,0:T(8,128)}, f32[8,8,1024]{2,1,0:T(8,128)}, f32[8,8,1024]{2,1,0:T(8,128)}, f32[8,8,1024]{2,1,0:T(8,128)}, f32[8,8,1024]{2,1,0...) custom-call(s32[1]{0:T(128)} %bitcast.place_ref, ...), custom_call_target="tpu_custom_call" | custom-call | flops 125829120 | bytes 12582912 | tf_op jit(solution)/shard_map/pallas_call | solution.py:125
  21.0 2.2 collective-permute-start.2
  31.2 2.7 collective-permute-start.5
  33.8 1.9 collective-permute-start.6
  35.8 42.7 %collective-permute-done.4 = f32[8,8,1024]{2,1,0:T(8,128)S(1)} collective-permute-done((f32[8,8,1024]{2,1,0:T(8,128)}, f32[8,8,1024]{2,1,0:T(8,128)S(1)}, u32[]{:S(2)}, u32[]{:S(2)}) %collective-permute-start.4) | collective-permute-done | bytes 262176 | tf_op jit(solution)/shard_map/ppermute | solution.py:202
  78.5 8.8 %collective-permute-start.7 = (f32[8,8,1024]{2,1,0:T(8,128)}, f32[8,8,1024]{2,1,0:T(8,128)S(1)}, u32[]{:S(2)}, u32[]{:S(2)}) collective-permute-start(f32[8,8,1024]{2,1,0:T(8,128)} %get-tuple-element.27), channel_id=1, source_target_pairs={{0,24},{4,28},{8,0},{12,4},{16,8},{20,12},{24,16},{28,20},{1,25},{... | collective-permute-start | bytes 786440 | tf_op jit(solution)/shard_map/ppermute | solution.py:202
  87.3 5.6 %collective-permute-start.8 = (f32[8,8,1024]{2,1,0:T(8,128)}, f32[8,8,1024]{2,1,0:T(8,128)S(1)}, u32[]{:S(2)}, u32[]{:S(2)}) collective-permute-start(f32[8,8,1024]{2,1,0:T(8,128)} %get-tuple-element.28), channel_id=1, source_target_pairs={{0,28},{4,0},{8,4},{12,8},{16,12},{20,16},{24,20},{28,24},{1,29},{... | collective-permute-start | bytes 786440 | tf_op jit(solution)/shard_map/ppermute | solution.py:202
  93.6 5.5 %collective-permute-done.8 = f32[8,8,1024]{2,1,0:T(8,128)S(1)} collective-permute-done((f32[8,8,1024]{2,1,0:T(8,128)}, f32[8,8,1024]{2,1,0:T(8,128)S(1)}, u32[]{:S(2)}, u32[]{:S(2)}) %collective-permute-start.8) | collective-permute-done | bytes 262176 | tf_op jit(solution)/shard_map/ppermute | solution.py:202
  99.2 6.8 %fusion.18 = f32[8,64,512]{2,1,0:T(8,128)S(1)} fusion(s32[8,512]{1,0:T(8,128)S(1)} %bitcast.62, f32[64,8,1024]{2,1,0:T(8,128)S(1)} %constant_dynamic-update-slice_fusion, f32[8,512]{1,0:T(8,128)S(1)} %bitcast.63), kind=kOutput, calls=%fused_computation.19 | convolution fusion | flops 3225944064 | bytes 3178496 | tf_op jit(solution)/shard_map/erl,rlo->reo/dot_general | solution.py:162
  108.4 6.7 %fusion.12 = f32[64,1,8,8,128]{4,0,3,2,1:T(8,128)S(1)} fusion(f32[64,8,8,128]{3,1,2,0:T(8,128)S(1)} %bitcast.61, s32[8,8,64]{2,1,0:T(8,128)S(1)} %get-tuple-element.56, s32[8,8,64]{2,1,0:T(8,128)S(1)} %get-tuple-element.57, s32[8,8,64]{2,1,0:T(8,128)S(1)} %get-tuple-element.55, f32[8,8,64]{2,1,0:T(8,128)S(1)} %divide_multiply_fusion), kind=kOutput, calls=%fused_computation.15 | convolution fusion | flops 405274624 | bytes 4259840 | tf_op jit(solution)/shard_map/rbek,kfrbc->efrbc/dot_general | solution.py:190
  115.5 3.5 %broadcast_in_dim.4 = f32[8,3,64,1024]{3,2,1,0:T(8,128)} broadcast(f32[]{:T(128)} %constant.92.clone.1), dimensions={} | broadcast | bytes 6291460 | tf_op jit(solution)/shard_map/broadcast_in_dim | solution.py:263
  123.7 3.3 %collective-permute-start.21 = (f32[8,2,8,1024]{3,2,1,0:T(8,128)S(1)}, f32[8,2,8,1024]{3,2,1,0:T(8,128)S(1)}, u32[]{:S(2)}, u32[]{:S(2)}) collective-permute-start(f32[8,2,8,1024]{3,2,1,0:T(8,128)S(1)} %copy-done.6), channel_id=1, source_target_pairs={{0,24},{4,28},{8,0},{12,4},{16,8},{20,12},{24,16},{28,20},{1,25},{... | collective-permute-start | bytes 1572872 | tf_op jit(solution)/shard_map/ppermute | solution.py:202
  129.1 2.3 collective-permute-done.19
  132.7 31.2 %collective-permute-start.11 = (f32[8,1,8,1024]{3,1,2,0:T(1,128)}, f32[8,1,8,1024]{3,1,2,0:T(1,128)}, u32[]{:S(2)}, u32[]{:S(2)}) collective-permute-start(f32[8,1,8,1024]{3,1,2,0:T(1,128)} %bitcast.15), channel_id=1, source_target_pairs={{0,24},{4,28},{8,0},{12,4},{16,8},{20,12},{24,16},{28,20},{1,25},{... | collective-permute-start | bytes 786440 | tf_op jit(solution)/shard_map/ppermute | solution.py:202
  164.0 28.0 %collective-permute-start.12 = (f32[8,1,8,1024]{3,1,2,0:T(1,128)}, f32[8,1,8,1024]{3,1,2,0:T(1,128)}, u32[]{:S(2)}, u32[]{:S(2)}) collective-permute-start(f32[8,1,8,1024]{3,1,2,0:T(1,128)} %bitcast.16), channel_id=1, source_target_pairs={{0,8},{4,12},{8,16},{12,20},{16,24},{20,28},{24,0},{28,4},{1,9},{5... | collective-permute-start | bytes 786440 | tf_op jit(solution)/shard_map/ppermute | solution.py:202
  192.0 4.3 %collective-permute-start.13 = (f32[8,1,8,1024]{3,1,2,0:T(1,128)}, f32[8,1,8,1024]{3,1,2,0:T(1,128)S(1)}, u32[]{:S(2)}, u32[]{:S(2)}) collective-permute-start(f32[8,1,8,1024]{3,1,2,0:T(1,128)} %bitcast.17), channel_id=1, source_target_pairs={{0,20},{4,24},{8,28},{12,0},{16,4},{20,8},{24,12},{28,16},{1,21},{... | collective-permute-start | bytes 786440 | tf_op jit(solution)/shard_map/ppermute | solution.py:202
  196.4 9.1 %fusion.5 = f32[64,2,8,8,128]{4,0,1,3,2:T(8,128)S(1)} fusion(f32[64,2,8,8,128]{4,2,3,1,0:T(8,128)S(1)} %bitcast.60, s32[8,8,64]{2,1,0:T(8,128)S(1)} %get-tuple-element.56, s32[8,8,64]{2,1,0:T(8,128)S(1)} %get-tuple-element.57, s32[8,8,64]{2,1,0:T(8,128)S(1)} %get-tuple-element.55, f32[8,8,64]{2,1,0:T(8,128)S(1)} %divide_multiply_fusion), kind=kOutput, calls=%fused_computation.6 | convolution fusion | flops 807927808 | bytes 8454144 | tf_op jit(solution)/shard_map/rbek,kfrbc->efrbc/dot_general | solution.py:190
  207.7 3.8 %collective-permute-start.15 = (f32[8,1,8,1024]{3,1,2,0:T(1,128)}, f32[8,1,8,1024]{3,1,2,0:T(1,128)}, u32[]{:S(2)}, u32[]{:S(2)}) collective-permute-start(f32[8,1,8,1024]{3,1,2,0:T(1,128)} %bitcast.19), channel_id=1, source_target_pairs={{0,16},{4,20},{8,24},{12,28},{16,0},{20,4},{24,8},{28,12},{1,17},{... | collective-permute-start | bytes 786440 | tf_op jit(solution)/shard_map/ppermute | solution.py:202
  213.2 1.9 slice.133
  215.1 2.0 copy.31
  217.1 1.9 slice.135
  219.1 3.3 %collective-permute-start.23 = (f32[8,2,8,1024]{3,2,1,0:T(8,128)}, f32[8,2,8,1024]{3,2,1,0:T(8,128)}, u32[]{:S(2)}, u32[]{:S(2)}) collective-permute-start(f32[8,2,8,1024]{3,2,1,0:T(8,128)} %slice.135), channel_id=1, source_target_pairs={{0,28},{4,0},{8,4},{12,8},{16,12},{20,16},{24,20},{28,24},{1,29},{... | collective-permute-start | bytes 1572872 | tf_op jit(solution)/shard_map/ppermute | solution.py:202
  225.0 1.9 slice.137
  229.7 1.9 slice.139
  237.4 8.5 %collective-permute-start.27 = (f32[8,2,8,1024]{3,2,1,0:T(8,128)S(1)}, f32[8,2,8,1024]{3,2,1,0:T(8,128)}, u32[]{:S(2)}, u32[]{:S(2)}) collective-permute-start(f32[8,2,8,1024]{3,2,1,0:T(8,128)S(1)} %slice.143), channel_id=1, source_target_pairs={{0,20},{4,24},{8,28},{12,0},{16,4},{20,8},{24,12},{28,16},{1,21},{... | collective-permute-start | bytes 1572872 | tf_op jit(solution)/shard_map/ppermute | solution.py:202
  249.1 1.9 constant_dynamic-update-slice_fusion.22
  251.0 8.6 %collective-permute-start.29 = (f32[8,2,8,1024]{3,2,1,0:T(8,128)S(1)}, f32[8,2,8,1024]{3,2,1,0:T(8,128)S(1)}, u32[]{:S(2)}, u32[]{:S(2)}) collective-permute-start(f32[8,2,8,1024]{3,2,1,0:T(8,128)S(1)} %slice.147), channel_id=1, source_target_pairs={{0,16},{4,20},{8,24},{12,28},{16,0},{20,4},{24,8},{28,12},{1,17},{... | collective-permute-start | bytes 1572872 | tf_op jit(solution)/shard_map/ppermute | solution.py:202
  261.4 1.9 constant_dynamic-update-slice_fusion.20
  265.2 14.3 %collective-permute-done.27 = f32[8,2,8,1024]{3,2,1,0:T(8,128)} collective-permute-done((f32[8,2,8,1024]{3,2,1,0:T(8,128)S(1)}, f32[8,2,8,1024]{3,2,1,0:T(8,128)}, u32[]{:S(2)}, u32[]{:S(2)}) %collective-permute-start.27) | collective-permute-done | bytes 524320 | tf_op jit(solution)/shard_map/ppermute | solution.py:202
  281.4 32.3 %collective-permute-done.28 = f32[8,2,8,1024]{3,2,1,0:T(8,128)S(1)} collective-permute-done((f32[8,2,8,1024]{3,2,1,0:T(8,128)S(1)}, f32[8,2,8,1024]{3,2,1,0:T(8,128)S(1)}, u32[]{:S(2)}, u32[]{:S(2)}) %collective-permute-start.28) | collective-permute-done | bytes 524320 | tf_op jit(solution)/shard_map/ppermute | solution.py:202
  314.5 4.0 %collective-permute-done.29 = f32[8,2,8,1024]{3,2,1,0:T(8,128)S(1)} collective-permute-done((f32[8,2,8,1024]{3,2,1,0:T(8,128)S(1)}, f32[8,2,8,1024]{3,2,1,0:T(8,128)S(1)}, u32[]{:S(2)}, u32[]{:S(2)}) %collective-permute-start.29) | collective-permute-done | bytes 524320 | tf_op jit(solution)/shard_map/ppermute | solution.py:202
  (125 shorter events, 53.1 us)
Async XLA Ops:
  1.6 7.8 %collective-permute-start = (f32[8,3,4,1024]{3,2,1,0:T(4,128)S(1)}, f32[8,3,4,1024]{3,2,1,0:T(4,128)S(1)}, u32[]{:S(2)}, u32[]{:S(2)}) collective-permute-start(f32[8,3,4,1024]{3,2,1,0:T(4,128)S(1)} %get-tuple-element.38), channel_id=1, source_target_pairs={{0,1},{1,2},{2,3},{4,5},{5,6},{6,7},{8,9},{9,10},{10,11},{12,13},{... | collective-permute-start | bytes 1179656 | tf_op jit(solution)/shard_map/ppermute | solution.py:31
  4.0 5.7 %collective-permute-start.1 = (f32[8,3,4,1024]{3,2,1,0:T(4,128)S(1)}, f32[8,3,4,1024]{3,2,1,0:T(4,128)S(1)}, u32[]{:S(2)}, u32[]{:S(2)}) collective-permute-start(f32[8,3,4,1024]{3,2,1,0:T(4,128)S(1)} %get-tuple-element.37), channel_id=1, source_target_pairs={{1,0},{2,1},{3,2},{5,4},{6,5},{7,6},{9,8},{10,9},{11,10},{13,12},{... | collective-permute-start | bytes 1179656 | tf_op jit(solution)/shard_map/ppermute | solution.py:32
  21.0 78.2 %copy-start.3 = (s32[1,8,512]{2,1,0:T(8,128)S(1)}, s32[1,8,512]{2,1,0:T(8,128)}, u32[]{:S(2)}) copy-start(s32[1,8,512]{2,1,0:T(8,128)} %param.7) | copy-start | bytes 49156
  21.0 78.2 %copy-start.9 = (f32[1,8,512]{2,1,0:T(8,128)S(1)}, f32[1,8,512]{2,1,0:T(8,128)}, u32[]{:S(2)}) copy-start(f32[1,8,512]{2,1,0:T(8,128)} %param.8) | copy-start | bytes 49156
  21.0 10.2 %collective-permute-start.2 = (f32[8,8,1024]{2,1,0:T(8,128)}, f32[8,8,1024]{2,1,0:T(8,128)S(1)}, u32[]{:S(2)}, u32[]{:S(2)}) collective-permute-start(f32[8,8,1024]{2,1,0:T(8,128)} %get-tuple-element.22), channel_id=1, source_target_pairs={{0,4},{4,8},{8,12},{12,16},{16,20},{20,24},{24,28},{28,0},{1,5},{5... | collective-permute-start | bytes 786440 | tf_op jit(solution)/shard_map/ppermute | solution.py:202
  23.2 10.6 %collective-permute-start.3 = (f32[8,8,1024]{2,1,0:T(8,128)}, f32[8,8,1024]{2,1,0:T(8,128)S(1)}, u32[]{:S(2)}, u32[]{:S(2)}) collective-permute-start(f32[8,8,1024]{2,1,0:T(8,128)} %get-tuple-element.23), channel_id=1, source_target_pairs={{0,8},{4,12},{8,16},{12,20},{16,24},{20,28},{24,0},{28,4},{1,9},{5... | collective-permute-start | bytes 786440 | tf_op jit(solution)/shard_map/ppermute | solution.py:202
  25.8 97.8 %collective-permute-start.16 = (f32[8,2,8,1024]{3,2,1,0:T(8,128)}, f32[8,2,8,1024]{3,2,1,0:T(8,128)S(1)}, u32[]{:S(2)}, u32[]{:S(2)}) collective-permute-start(f32[8,2,8,1024]{3,2,1,0:T(8,128)} %get-tuple-element.30), channel_id=1, source_target_pairs={{0,4},{4,8},{8,12},{12,16},{16,20},{20,24},{24,28},{28,0},{1,5},{5... | collective-permute-start | bytes 1572872 | tf_op jit(solution)/shard_map/ppermute | solution.py:202
  27.4 99.7 %collective-permute-start.17 = (f32[8,2,8,1024]{3,2,1,0:T(8,128)}, f32[8,2,8,1024]{3,2,1,0:T(8,128)S(1)}, u32[]{:S(2)}, u32[]{:S(2)}) collective-permute-start(f32[8,2,8,1024]{3,2,1,0:T(8,128)} %get-tuple-element.31), channel_id=1, source_target_pairs={{0,8},{4,12},{8,16},{12,20},{16,24},{20,28},{24,0},{28,4},{1,9},{5... | collective-permute-start | bytes 1572872 | tf_op jit(solution)/shard_map/ppermute | solution.py:202
  29.0 49.5 %collective-permute-start.4 = (f32[8,8,1024]{2,1,0:T(8,128)}, f32[8,8,1024]{2,1,0:T(8,128)S(1)}, u32[]{:S(2)}, u32[]{:S(2)}) collective-permute-start(f32[8,8,1024]{2,1,0:T(8,128)} %get-tuple-element.24), channel_id=1, source_target_pairs={{0,12},{4,16},{8,20},{12,24},{16,28},{20,0},{24,4},{28,8},{1,13},{... | collective-permute-start | bytes 786440 | tf_op jit(solution)/shard_map/ppermute | solution.py:202
  31.2 56.1 %collective-permute-start.5 = (f32[8,8,1024]{2,1,0:T(8,128)}, f32[8,8,1024]{2,1,0:T(8,128)S(1)}, u32[]{:S(2)}, u32[]{:S(2)}) collective-permute-start(f32[8,8,1024]{2,1,0:T(8,128)} %get-tuple-element.25), channel_id=1, source_target_pairs={{0,16},{4,20},{8,24},{12,28},{16,0},{20,4},{24,8},{28,12},{1,17},{... | collective-permute-start | bytes 786440 | tf_op jit(solution)/shard_map/ppermute | solution.py:202
  33.8 59.0 %collective-permute-start.6 = (f32[8,8,1024]{2,1,0:T(8,128)}, f32[8,8,1024]{2,1,0:T(8,128)S(1)}, u32[]{:S(2)}, u32[]{:S(2)}) collective-permute-start(f32[8,8,1024]{2,1,0:T(8,128)} %get-tuple-element.26), channel_id=1, source_target_pairs={{0,20},{4,24},{8,28},{12,0},{16,4},{20,8},{24,12},{28,16},{1,21},{... | collective-permute-start | bytes 786440 | tf_op jit(solution)/shard_map/ppermute | solution.py:202
  78.5 14.5 %collective-permute-start.7 = (f32[8,8,1024]{2,1,0:T(8,128)}, f32[8,8,1024]{2,1,0:T(8,128)S(1)}, u32[]{:S(2)}, u32[]{:S(2)}) collective-permute-start(f32[8,8,1024]{2,1,0:T(8,128)} %get-tuple-element.27), channel_id=1, source_target_pairs={{0,24},{4,28},{8,0},{12,4},{16,8},{20,12},{24,16},{28,20},{1,25},{... | collective-permute-start | bytes 786440 | tf_op jit(solution)/shard_map/ppermute | solution.py:202
  87.3 11.9 %collective-permute-start.8 = (f32[8,8,1024]{2,1,0:T(8,128)}, f32[8,8,1024]{2,1,0:T(8,128)S(1)}, u32[]{:S(2)}, u32[]{:S(2)}) collective-permute-start(f32[8,8,1024]{2,1,0:T(8,128)} %get-tuple-element.28), channel_id=1, source_target_pairs={{0,28},{4,0},{8,4},{12,8},{16,12},{20,16},{24,20},{28,24},{1,29},{... | collective-permute-start | bytes 786440 | tf_op jit(solution)/shard_map/ppermute | solution.py:202
  92.9 36.1 %collective-permute-start.18 = (f32[8,2,8,1024]{3,2,1,0:T(8,128)}, f32[8,2,8,1024]{3,2,1,0:T(8,128)S(1)}, u32[]{:S(2)}, u32[]{:S(2)}) collective-permute-start(f32[8,2,8,1024]{3,2,1,0:T(8,128)} %get-tuple-element.32), channel_id=1, source_target_pairs={{0,12},{4,16},{8,20},{12,24},{16,28},{20,0},{24,4},{28,8},{1,13},{... | collective-permute-start | bytes 1572872 | tf_op jit(solution)/shard_map/ppermute | solution.py:202
  93.0 38.4 %collective-permute-start.19 = (f32[8,2,8,1024]{3,2,1,0:T(8,128)S(1)}, f32[8,2,8,1024]{3,2,1,0:T(8,128)S(1)}, u32[]{:S(2)}, u32[]{:S(2)}) collective-permute-start(f32[8,2,8,1024]{3,2,1,0:T(8,128)S(1)} %copy-done.8), channel_id=1, source_target_pairs={{0,16},{4,20},{8,24},{12,28},{16,0},{20,4},{24,8},{28,12},{1,17},{... | collective-permute-start | bytes 1572872 | tf_op jit(solution)/shard_map/ppermute | solution.py:202
  99.1 33.6 %collective-permute-start.20 = (f32[8,2,8,1024]{3,2,1,0:T(8,128)S(1)}, f32[8,2,8,1024]{3,2,1,0:T(8,128)S(1)}, u32[]{:S(2)}, u32[]{:S(2)}) collective-permute-start(f32[8,2,8,1024]{3,2,1,0:T(8,128)S(1)} %copy-done.7), channel_id=1, source_target_pairs={{0,20},{4,24},{8,28},{12,0},{16,4},{20,8},{24,12},{28,16},{1,21},{... | collective-permute-start | bytes 1572872 | tf_op jit(solution)/shard_map/ppermute | solution.py:202
  123.7 40.3 %collective-permute-start.21 = (f32[8,2,8,1024]{3,2,1,0:T(8,128)S(1)}, f32[8,2,8,1024]{3,2,1,0:T(8,128)S(1)}, u32[]{:S(2)}, u32[]{:S(2)}) collective-permute-start(f32[8,2,8,1024]{3,2,1,0:T(8,128)S(1)} %copy-done.6), channel_id=1, source_target_pairs={{0,24},{4,28},{8,0},{12,4},{16,8},{20,12},{24,16},{28,20},{1,25},{... | collective-permute-start | bytes 1572872 | tf_op jit(solution)/shard_map/ppermute | solution.py:202
  127.1 64.9 %collective-permute-start.22 = (f32[8,2,8,1024]{3,2,1,0:T(8,128)S(1)}, f32[8,2,8,1024]{3,2,1,0:T(8,128)S(1)}, u32[]{:S(2)}, u32[]{:S(2)}) collective-permute-start(f32[8,2,8,1024]{3,2,1,0:T(8,128)S(1)} %copy-done.5), channel_id=1, source_target_pairs={{0,28},{4,0},{8,4},{12,8},{16,12},{20,16},{24,20},{28,24},{1,29},{... | collective-permute-start | bytes 1572872 | tf_op jit(solution)/shard_map/ppermute | solution.py:202
  129.0 77.9 %collective-permute-start.9 = (f32[8,1,8,1024]{3,1,2,0:T(1,128)S(1)}, f32[8,1,8,1024]{3,1,2,0:T(1,128)S(1)}, u32[]{:S(2)}, u32[]{:S(2)}) collective-permute-start(f32[8,1,8,1024]{3,1,2,0:T(1,128)S(1)} %bitcast.59), channel_id=1, source_target_pairs={{0,28},{4,0},{8,4},{12,8},{16,12},{20,16},{24,20},{28,24},{1,29},{... | collective-permute-start | bytes 786440 | tf_op jit(solution)/shard_map/ppermute | solution.py:202
  131.4 76.3 %collective-permute-start.10 = (f32[8,1,8,1024]{3,1,2,0:T(1,128)S(1)}, f32[8,1,8,1024]{3,1,2,0:T(1,128)S(1)}, u32[]{:S(2)}, u32[]{:S(2)}) collective-permute-start(f32[8,1,8,1024]{3,1,2,0:T(1,128)S(1)} %bitcast.58), channel_id=1, source_target_pairs={{0,4},{4,8},{8,12},{12,16},{16,20},{20,24},{24,28},{28,0},{1,5},{5... | collective-permute-start | bytes 786440 | tf_op jit(solution)/shard_map/ppermute | solution.py:202
  132.7 86.4 %collective-permute-start.11 = (f32[8,1,8,1024]{3,1,2,0:T(1,128)}, f32[8,1,8,1024]{3,1,2,0:T(1,128)}, u32[]{:S(2)}, u32[]{:S(2)}) collective-permute-start(f32[8,1,8,1024]{3,1,2,0:T(1,128)} %bitcast.15), channel_id=1, source_target_pairs={{0,24},{4,28},{8,0},{12,4},{16,8},{20,12},{24,16},{28,20},{1,25},{... | collective-permute-start | bytes 786440 | tf_op jit(solution)/shard_map/ppermute | solution.py:202
  164.0 63.0 %collective-permute-start.12 = (f32[8,1,8,1024]{3,1,2,0:T(1,128)}, f32[8,1,8,1024]{3,1,2,0:T(1,128)}, u32[]{:S(2)}, u32[]{:S(2)}) collective-permute-start(f32[8,1,8,1024]{3,1,2,0:T(1,128)} %bitcast.16), channel_id=1, source_target_pairs={{0,8},{4,12},{8,16},{12,20},{16,24},{20,28},{24,0},{28,4},{1,9},{5... | collective-permute-start | bytes 786440 | tf_op jit(solution)/shard_map/ppermute | solution.py:202
  192.0 39.5 %collective-permute-start.13 = (f32[8,1,8,1024]{3,1,2,0:T(1,128)}, f32[8,1,8,1024]{3,1,2,0:T(1,128)S(1)}, u32[]{:S(2)}, u32[]{:S(2)}) collective-permute-start(f32[8,1,8,1024]{3,1,2,0:T(1,128)} %bitcast.17), channel_id=1, source_target_pairs={{0,20},{4,24},{8,28},{12,0},{16,4},{20,8},{24,12},{28,16},{1,21},{... | collective-permute-start | bytes 786440 | tf_op jit(solution)/shard_map/ppermute | solution.py:202
  206.9 27.6 %collective-permute-start.14 = (f32[8,1,8,1024]{3,1,2,0:T(1,128)}, f32[8,1,8,1024]{3,1,2,0:T(1,128)}, u32[]{:S(2)}, u32[]{:S(2)}) collective-permute-start(f32[8,1,8,1024]{3,1,2,0:T(1,128)} %bitcast.18), channel_id=1, source_target_pairs={{0,12},{4,16},{8,20},{12,24},{16,28},{20,0},{24,4},{28,8},{1,13},{... | collective-permute-start | bytes 786440 | tf_op jit(solution)/shard_map/ppermute | solution.py:202
  207.7 29.7 %collective-permute-start.15 = (f32[8,1,8,1024]{3,1,2,0:T(1,128)}, f32[8,1,8,1024]{3,1,2,0:T(1,128)}, u32[]{:S(2)}, u32[]{:S(2)}) collective-permute-start(f32[8,1,8,1024]{3,1,2,0:T(1,128)} %bitcast.19), channel_id=1, source_target_pairs={{0,16},{4,20},{8,24},{12,28},{16,0},{20,4},{24,8},{28,12},{1,17},{... | collective-permute-start | bytes 786440 | tf_op jit(solution)/shard_map/ppermute | solution.py:202
  219.1 29.9 %collective-permute-start.23 = (f32[8,2,8,1024]{3,2,1,0:T(8,128)}, f32[8,2,8,1024]{3,2,1,0:T(8,128)}, u32[]{:S(2)}, u32[]{:S(2)}) collective-permute-start(f32[8,2,8,1024]{3,2,1,0:T(8,128)} %slice.135), channel_id=1, source_target_pairs={{0,28},{4,0},{8,4},{12,8},{16,12},{20,16},{24,20},{28,24},{1,29},{... | collective-permute-start | bytes 1572872 | tf_op jit(solution)/shard_map/ppermute | solution.py:202
  226.9 24.0 %collective-permute-start.24 = (f32[8,2,8,1024]{3,2,1,0:T(8,128)}, f32[8,2,8,1024]{3,2,1,0:T(8,128)}, u32[]{:S(2)}, u32[]{:S(2)}) collective-permute-start(f32[8,2,8,1024]{3,2,1,0:T(8,128)} %slice.137), channel_id=1, source_target_pairs={{0,4},{4,8},{8,12},{12,16},{16,20},{20,24},{24,28},{28,0},{1,5},{5... | collective-permute-start | bytes 1572872 | tf_op jit(solution)/shard_map/ppermute | solution.py:202
  231.6 29.9 %collective-permute-start.25 = (f32[8,2,8,1024]{3,2,1,0:T(8,128)}, f32[8,2,8,1024]{3,2,1,0:T(8,128)}, u32[]{:S(2)}, u32[]{:S(2)}) collective-permute-start(f32[8,2,8,1024]{3,2,1,0:T(8,128)} %slice.139), channel_id=1, source_target_pairs={{0,24},{4,28},{8,0},{12,4},{16,8},{20,12},{24,16},{28,20},{1,25},{... | collective-permute-start | bytes 1572872 | tf_op jit(solution)/shard_map/ppermute | solution.py:202
  234.5 28.9 %collective-permute-start.26 = (f32[8,2,8,1024]{3,2,1,0:T(8,128)}, f32[8,2,8,1024]{3,2,1,0:T(8,128)}, u32[]{:S(2)}, u32[]{:S(2)}) collective-permute-start(f32[8,2,8,1024]{3,2,1,0:T(8,128)} %slice.141), channel_id=1, source_target_pairs={{0,8},{4,12},{8,16},{12,20},{16,24},{20,28},{24,0},{28,4},{1,9},{5... | collective-permute-start | bytes 1572872 | tf_op jit(solution)/shard_map/ppermute | solution.py:202
  237.4 42.1 %collective-permute-start.27 = (f32[8,2,8,1024]{3,2,1,0:T(8,128)S(1)}, f32[8,2,8,1024]{3,2,1,0:T(8,128)}, u32[]{:S(2)}, u32[]{:S(2)}) collective-permute-start(f32[8,2,8,1024]{3,2,1,0:T(8,128)S(1)} %slice.143), channel_id=1, source_target_pairs={{0,20},{4,24},{8,28},{12,0},{16,4},{20,8},{24,12},{28,16},{1,21},{... | collective-permute-start | bytes 1572872 | tf_op jit(solution)/shard_map/ppermute | solution.py:202
  249.0 64.7 %collective-permute-start.28 = (f32[8,2,8,1024]{3,2,1,0:T(8,128)S(1)}, f32[8,2,8,1024]{3,2,1,0:T(8,128)S(1)}, u32[]{:S(2)}, u32[]{:S(2)}) collective-permute-start(f32[8,2,8,1024]{3,2,1,0:T(8,128)S(1)} %slice.145), channel_id=1, source_target_pairs={{0,12},{4,16},{8,20},{12,24},{16,28},{20,0},{24,4},{28,8},{1,13},{... | collective-permute-start | bytes 1572872 | tf_op jit(solution)/shard_map/ppermute | solution.py:202
  251.0 67.5 %collective-permute-start.29 = (f32[8,2,8,1024]{3,2,1,0:T(8,128)S(1)}, f32[8,2,8,1024]{3,2,1,0:T(8,128)S(1)}, u32[]{:S(2)}, u32[]{:S(2)}) collective-permute-start(f32[8,2,8,1024]{3,2,1,0:T(8,128)S(1)} %slice.147), channel_id=1, source_target_pairs={{0,16},{4,20},{8,24},{12,28},{16,0},{20,4},{24,8},{28,12},{1,17},{... | collective-permute-start | bytes 1572872 | tf_op jit(solution)/shard_map/ppermute | solution.py:202
  (8 other events, 195.2 us)

commit v2 on v1

--- a/solution.py
+++ b/solution.py
@@ -197,10 +197,12 @@
 
 def send_all(pieces, axis):
     count = lax.axis_size(axis)
-    received = {0: pieces[0]}
-    for d in by_reach(count):
-        received[d] = lax.ppermute(pieces[d], axis, [(i, (i + d) % count) for i in range(count)])
-    return [received[d] for d in range(count)]
+    received = [
+        lax.ppermute(pieces[d], axis, [(i, (i + d) % count) for i in range(count)])
+        for d in range(1, count)
+    ]
+    own, first = lax.optimization_barrier((pieces[0], received[0]))
+    return [own, first] + received[1:]
 
 
 def row_pieces(array, axis, dim):

time: 324 us -> 323 us (level); the launches traced: 319 us -> 322 us
  waiting for transfers between devices: 101 us -> 113 us
  starting transfers between devices: 128 us -> 123 us
    ppermute x28, waiting for transfers between devices: 101 us -> 112 us  [send_all(): lax.ppermute(pieces[d], axis, [(i, (i + d) % count) for i in range(count)])]
    ppermute x28, starting transfers between devices: 124 us -> 120 us  [send_all(): lax.ppermute(pieces[d], axis, [(i, (i + d) % count) for i in range(count)])]
  transfers between devices with their start and end apart: 30 -> 30, of which waited for: 7 -> 10; matrix products, arithmetic and copies ran while one was open for 24% -> 22% of each run, Pallas kernels for 0% -> 0%
where the time goes in v2:
time: 323 us; the launch traced here: 322 us
  starting transfers between devices  123 us (38%)
  waiting for transfers between devices  113 us (35%)
  local copies, waits for them, and re-layouts  48.6 us (15%)
  matrix products  23.7 us (7%)
  Pallas kernels  10.5 us (3%)
  other arithmetic  3.25 us (1%)
    ppermute x28, starting transfers between devices, send_all(): lax.ppermute(pieces[d], axis, [(i, (i + d) % count) for i in range(count)])  120 us
    ppermute x28, waiting for transfers between devices, send_all(): lax.ppermute(pieces[d], axis, [(i, (i + d) % count) for i in range(count)])  112 us
    dynamic_update_slice x16, local copies, waits for them, and re-layouts, put_back(): whole = lax.dynamic_update_slice(whole, piece, (0, field, start, 0))  21.7 us
    slice x26, local copies, waits for them, and re-layouts, hand_back(): updated[d * members_dev:(d + 1) * members_dev]  18.1 us
    dot_general x2, matrix products, merge_fields(): jnp.einsum('rbek,kfrbc->efrbc', mixing, blocks, precision=lax.Precision.H...  15.9 us
    pallas_call x1, Pallas kernels, forecast_pieces(): pl.pallas_call(functools.partial(forecast_kernel, count), grid=(members,)...  10.5 us
    dot_general x1, matrix products, member_weights(): jnp.einsum('erl,rlo->reo', heights, chosen_cells, precision=lax.Precision...  6.8 us
  transfers between devices with their start and end apart: 30, of which 10 were waited for; matrix products, arithmetic and copies ran while one was open for 22% of the time, Pallas kernels for 0%

profile of v2, /device:TPU:0, one launch (start us, length us, event | category | flops | bytes accessed | tf_op | source)
XLA Modules:
  0.0 322.4 jit_solution(311194606028225766)
XLA Ops:
  1.6 2.4 collective-permute-start
  10.5 10.5 %shard_map.55 = (f32[8,8,1024]{2,1,0:T(8,128)}, f32[8,8,1024]{2,1,0:T(8,128)}, f32[8,8,1024]{2,1,0:T(8,128)}, f32[8,8,1024]{2,1,0:T(8,128)}, f32[8,8,1024]{2,1,0...) custom-call(s32[1]{0:T(128)} %bitcast.place_ref, ...), custom_call_target="tpu_custom_call" | custom-call | flops 125829120 | bytes 12582912 | tf_op jit(solution)/shard_map/pallas_call | solution.py:125
  32.1 2.4 collective-permute-start.6
  34.5 43.5 %collective-permute-done.4 = f32[8,8,1024]{2,1,0:T(8,128)S(1)} collective-permute-done((f32[8,8,1024]{2,1,0:T(8,128)}, f32[8,8,1024]{2,1,0:T(8,128)S(1)}, u32[]{:S(2)}, u32[]{:S(2)}) %collective-permute-start.4) | collective-permute-done | bytes 262176 | tf_op jit(solution)/shard_map/ppermute | solution.py:201
  78.0 8.0 %collective-permute-start.7 = (f32[8,8,1024]{2,1,0:T(8,128)}, f32[8,8,1024]{2,1,0:T(8,128)S(1)}, u32[]{:S(2)}, u32[]{:S(2)}) collective-permute-start(f32[8,8,1024]{2,1,0:T(8,128)} %get-tuple-element.37), channel_id=1, source_target_pairs={{0,24},{4,28},{8,0},{12,4},{16,8},{20,12},{24,16},{28,20},{1,25},{... | collective-permute-start | bytes 786440 | tf_op jit(solution)/shard_map/ppermute | solution.py:201
  86.0 5.6 %collective-permute-start.8 = (f32[8,8,1024]{2,1,0:T(8,128)}, f32[8,8,1024]{2,1,0:T(8,128)S(1)}, u32[]{:S(2)}, u32[]{:S(2)}) collective-permute-start(f32[8,8,1024]{2,1,0:T(8,128)} %get-tuple-element.38), channel_id=1, source_target_pairs={{0,28},{4,0},{8,4},{12,8},{16,12},{20,16},{24,20},{28,24},{1,29},{... | collective-permute-start | bytes 786440 | tf_op jit(solution)/shard_map/ppermute | solution.py:201
  92.3 4.3 %collective-permute-done.8 = f32[8,8,1024]{2,1,0:T(8,128)S(1)} collective-permute-done((f32[8,8,1024]{2,1,0:T(8,128)}, f32[8,8,1024]{2,1,0:T(8,128)S(1)}, u32[]{:S(2)}, u32[]{:S(2)}) %collective-permute-start.8) | collective-permute-done | bytes 262176 | tf_op jit(solution)/shard_map/ppermute | solution.py:201
  96.6 6.8 %fusion.18 = f32[8,64,512]{2,1,0:T(8,128)S(1)} fusion(s32[8,512]{1,0:T(8,128)S(1)} %bitcast.62, f32[64,8,1024]{2,1,0:T(8,128)S(1)} %constant_dynamic-update-slice_fusion, f32[8,512]{1,0:T(8,128)S(1)} %bitcast.63), kind=kOutput, calls=%fused_computation.19 | convolution fusion | flops 3225944064 | bytes 3178496 | tf_op jit(solution)/shard_map/erl,rlo->reo/dot_general | solution.py:162
  105.9 6.8 %fusion.12 = f32[64,1,8,8,128]{4,0,3,2,1:T(8,128)S(1)} fusion(f32[64,8,8,128]{3,1,2,0:T(8,128)S(1)} %bitcast.61, s32[8,8,64]{2,1,0:T(8,128)S(1)} %get-tuple-element.72, s32[8,8,64]{2,1,0:T(8,128)S(1)} %get-tuple-element.73, s32[8,8,64]{2,1,0:T(8,128)S(1)} %get-tuple-element.71, f32[8,8,64]{2,1,0:T(8,128)S(1)} %divide_multiply_fusion), kind=kOutput, calls=%fused_computation.15 | convolution fusion | flops 405274624 | bytes 4259840 | tf_op jit(solution)/shard_map/rbek,kfrbc->efrbc/dot_general | solution.py:190
  116.9 5.9 %collective-permute-start.21 = (f32[8,2,8,1024]{3,2,1,0:T(8,128)S(1)}, f32[8,2,8,1024]{3,2,1,0:T(8,128)S(1)}, u32[]{:S(2)}, u32[]{:S(2)}) collective-permute-start(f32[8,2,8,1024]{3,2,1,0:T(8,128)S(1)} %copy-done.7), channel_id=1, source_target_pairs={{0,24},{4,28},{8,0},{12,4},{16,8},{20,12},{24,16},{28,20},{1,25},{... | collective-permute-start | bytes 1572872 | tf_op jit(solution)/shard_map/ppermute | solution.py:201
  123.0 2.1 collective-permute-start.9
  125.1 4.9 %collective-permute-done.19 = f32[8,2,8,1024]{3,2,1,0:T(8,128)S(1)} collective-permute-done((f32[8,2,8,1024]{3,2,1,0:T(8,128)}, f32[8,2,8,1024]{3,2,1,0:T(8,128)S(1)}, u32[]{:S(2)}, u32[]{:S(2)}) %collective-permute-start.19) | collective-permute-done | bytes 524320 | tf_op jit(solution)/shard_map/ppermute | solution.py:201
  130.1 23.8 %collective-permute-start.10 = (f32[8,1,8,1024]{3,1,2,0:T(1,128)S(1)}, f32[8,1,8,1024]{3,1,2,0:T(1,128)S(1)}, u32[]{:S(2)}, u32[]{:S(2)}) collective-permute-start(f32[8,1,8,1024]{3,1,2,0:T(1,128)S(1)} %bitcast.58), channel_id=1, source_target_pairs={{0,28},{4,0},{8,4},{12,8},{16,12},{20,16},{24,20},{28,24},{1,29},{... | collective-permute-start | bytes 786440 | tf_op jit(solution)/shard_map/ppermute | solution.py:201
  154.0 4.2 %collective-permute-start.11 = (f32[8,1,8,1024]{3,1,2,0:T(1,128)}, f32[8,1,8,1024]{3,1,2,0:T(1,128)}, u32[]{:S(2)}, u32[]{:S(2)}) collective-permute-start(f32[8,1,8,1024]{3,1,2,0:T(1,128)} %bitcast.15), channel_id=1, source_target_pairs={{0,24},{4,28},{8,0},{12,4},{16,8},{20,12},{24,16},{28,20},{1,25},{... | collective-permute-start | bytes 786440 | tf_op jit(solution)/shard_map/ppermute | solution.py:201
  158.2 30.9 %collective-permute-start.12 = (f32[8,1,8,1024]{3,1,2,0:T(1,128)}, f32[8,1,8,1024]{3,1,2,0:T(1,128)}, u32[]{:S(2)}, u32[]{:S(2)}) collective-permute-start(f32[8,1,8,1024]{3,1,2,0:T(1,128)} %bitcast.16), channel_id=1, source_target_pairs={{0,8},{4,12},{8,16},{12,20},{16,24},{20,28},{24,0},{28,4},{1,9},{5... | collective-permute-start | bytes 786440 | tf_op jit(solution)/shard_map/ppermute | solution.py:201
  189.2 4.2 %collective-permute-start.13 = (f32[8,1,8,1024]{3,1,2,0:T(1,128)}, f32[8,1,8,1024]{3,1,2,0:T(1,128)S(1)}, u32[]{:S(2)}, u32[]{:S(2)}) collective-permute-start(f32[8,1,8,1024]{3,1,2,0:T(1,128)} %bitcast.17), channel_id=1, source_target_pairs={{0,20},{4,24},{8,28},{12,0},{16,4},{20,8},{24,12},{28,16},{1,21},{... | collective-permute-start | bytes 786440 | tf_op jit(solution)/shard_map/ppermute | solution.py:201
  193.5 9.1 %fusion.5 = f32[64,2,8,8,128]{4,0,1,3,2:T(8,128)S(1)} fusion(f32[64,2,8,8,128]{4,2,3,1,0:T(8,128)S(1)} %bitcast.60, s32[8,8,64]{2,1,0:T(8,128)S(1)} %get-tuple-element.72, s32[8,8,64]{2,1,0:T(8,128)S(1)} %get-tuple-element.73, s32[8,8,64]{2,1,0:T(8,128)S(1)} %get-tuple-element.71, f32[8,8,64]{2,1,0:T(8,128)S(1)} %divide_multiply_fusion), kind=kOutput, calls=%fused_computation.6 | convolution fusion | flops 807927808 | bytes 8454144 | tf_op jit(solution)/shard_map/rbek,kfrbc->efrbc/dot_general | solution.py:190
  204.0 3.5 %broadcast_in_dim.4 = f32[8,3,64,1024]{3,2,1,0:T(8,128)} broadcast(f32[]{:T(128)} %constant.92.clone.1), dimensions={} | broadcast | bytes 6291460 | tf_op jit(solution)/shard_map/broadcast_in_dim | solution.py:265
  208.2 3.8 %collective-permute-start.15 = (f32[8,1,8,1024]{3,1,2,0:T(1,128)}, f32[8,1,8,1024]{3,1,2,0:T(1,128)}, u32[]{:S(2)}, u32[]{:S(2)}) collective-permute-start(f32[8,1,8,1024]{3,1,2,0:T(1,128)} %bitcast.19), channel_id=1, source_target_pairs={{0,16},{4,20},{8,24},{12,28},{16,0},{20,4},{24,8},{28,12},{1,17},{... | collective-permute-start | bytes 786440 | tf_op jit(solution)/shard_map/ppermute | solution.py:201
  214.5 1.9 slice.135
  218.7 2.0 copy.30
  220.7 1.9 slice.133
  223.6 1.9 slice.137
  225.5 4.2 %collective-permute-start.24 = (f32[8,2,8,1024]{3,2,1,0:T(8,128)}, f32[8,2,8,1024]{3,2,1,0:T(8,128)}, u32[]{:S(2)}, u32[]{:S(2)}) collective-permute-start(f32[8,2,8,1024]{3,2,1,0:T(8,128)} %slice.137), channel_id=1, source_target_pairs={{0,28},{4,0},{8,4},{12,8},{16,12},{20,16},{24,20},{28,24},{1,29},{... | collective-permute-start | bytes 1572872 | tf_op jit(solution)/shard_map/ppermute | solution.py:201
  235.1 2.3 collective-permute-done.14
  239.1 3.4 %collective-permute-start.27 = (f32[8,2,8,1024]{3,2,1,0:T(8,128)S(1)}, f32[8,2,8,1024]{3,2,1,0:T(8,128)}, u32[]{:S(2)}, u32[]{:S(2)}) collective-permute-start(f32[8,2,8,1024]{3,2,1,0:T(8,128)S(1)} %slice.143), channel_id=1, source_target_pairs={{0,20},{4,24},{8,28},{12,0},{16,4},{20,8},{24,12},{28,16},{1,21},{... | collective-permute-start | bytes 1572872 | tf_op jit(solution)/shard_map/ppermute | solution.py:201
  244.7 9.0 %collective-permute-start.28 = (f32[8,2,8,1024]{3,2,1,0:T(8,128)S(1)}, f32[8,2,8,1024]{3,2,1,0:T(8,128)S(1)}, u32[]{:S(2)}, u32[]{:S(2)}) collective-permute-start(f32[8,2,8,1024]{3,2,1,0:T(8,128)S(1)} %slice.145), channel_id=1, source_target_pairs={{0,12},{4,16},{8,20},{12,24},{16,28},{20,0},{24,4},{28,8},{1,13},{... | collective-permute-start | bytes 1572872 | tf_op jit(solution)/shard_map/ppermute | solution.py:201
  254.6 1.9 collective-permute-start.29
  262.2 3.8 %collective-permute-done.26 = f32[8,2,8,1024]{3,2,1,0:T(8,128)} collective-permute-done((f32[8,2,8,1024]{3,2,1,0:T(8,128)}, f32[8,2,8,1024]{3,2,1,0:T(8,128)}, u32[]{:S(2)}, u32[]{:S(2)}) %collective-permute-start.26) | collective-permute-done | bytes 524320 | tf_op jit(solution)/shard_map/ppermute | solution.py:201
  267.8 9.3 %collective-permute-done.27 = f32[8,2,8,1024]{3,2,1,0:T(8,128)} collective-permute-done((f32[8,2,8,1024]{3,2,1,0:T(8,128)S(1)}, f32[8,2,8,1024]{3,2,1,0:T(8,128)}, u32[]{:S(2)}, u32[]{:S(2)}) %collective-permute-start.27) | collective-permute-done | bytes 524320 | tf_op jit(solution)/shard_map/ppermute | solution.py:201
  279.0 31.2 %collective-permute-done.28 = f32[8,2,8,1024]{3,2,1,0:T(8,128)S(1)} collective-permute-done((f32[8,2,8,1024]{3,2,1,0:T(8,128)S(1)}, f32[8,2,8,1024]{3,2,1,0:T(8,128)S(1)}, u32[]{:S(2)}, u32[]{:S(2)}) %collective-permute-start.28) | collective-permute-done | bytes 524320 | tf_op jit(solution)/shard_map/ppermute | solution.py:201
  311.1 10.6 %collective-permute-done.29 = f32[8,2,8,1024]{3,2,1,0:T(8,128)S(1)} collective-permute-done((f32[8,2,8,1024]{3,2,1,0:T(8,128)S(1)}, f32[8,2,8,1024]{3,2,1,0:T(8,128)S(1)}, u32[]{:S(2)}, u32[]{:S(2)}) %collective-permute-start.29) | collective-permute-done | bytes 524320 | tf_op jit(solution)/shard_map/ppermute | solution.py:201
  (123 shorter events, 55.9 us)
Async XLA Ops:
  1.6 7.1 %collective-permute-start = (f32[8,3,4,1024]{3,2,1,0:T(4,128)S(1)}, f32[8,3,4,1024]{3,2,1,0:T(4,128)S(1)}, u32[]{:S(2)}, u32[]{:S(2)}) collective-permute-start(f32[8,3,4,1024]{3,2,1,0:T(4,128)S(1)} %get-tuple-element.54), channel_id=1, source_target_pairs={{0,1},{1,2},{2,3},{4,5},{5,6},{6,7},{8,9},{9,10},{10,11},{12,13},{... | collective-permute-start | bytes 1179656 | tf_op jit(solution)/shard_map/ppermute | solution.py:31
  4.0 5.7 %collective-permute-start.1 = (f32[8,3,4,1024]{3,2,1,0:T(4,128)S(1)}, f32[8,3,4,1024]{3,2,1,0:T(4,128)S(1)}, u32[]{:S(2)}, u32[]{:S(2)}) collective-permute-start(f32[8,3,4,1024]{3,2,1,0:T(4,128)S(1)} %get-tuple-element.53), channel_id=1, source_target_pairs={{1,0},{2,1},{3,2},{5,4},{6,5},{7,6},{9,8},{10,9},{11,10},{13,12},{... | collective-permute-start | bytes 1179656 | tf_op jit(solution)/shard_map/ppermute | solution.py:32
  10.5 86.2 %copy-start.8 = (f32[1,8,512]{2,1,0:T(8,128)S(1)}, f32[1,8,512]{2,1,0:T(8,128)}, u32[]{:S(2)}) copy-start(f32[1,8,512]{2,1,0:T(8,128)} %param.8) | copy-start | bytes 49156
  20.9 9.3 %collective-permute-start.2 = (f32[8,8,1024]{2,1,0:T(8,128)}, f32[8,8,1024]{2,1,0:T(8,128)S(1)}, u32[]{:S(2)}, u32[]{:S(2)}) collective-permute-start(f32[8,8,1024]{2,1,0:T(8,128)} %get-tuple-element.30), channel_id=1, source_target_pairs={{0,4},{4,8},{8,12},{12,16},{16,20},{20,24},{24,28},{28,0},{1,5},{5... | collective-permute-start | bytes 786440 | tf_op jit(solution)/shard_map/ppermute | solution.py:201
  22.5 9.5 %collective-permute-start.3 = (f32[8,8,1024]{2,1,0:T(8,128)}, f32[8,8,1024]{2,1,0:T(8,128)S(1)}, u32[]{:S(2)}, u32[]{:S(2)}) collective-permute-start(f32[8,8,1024]{2,1,0:T(8,128)} %get-tuple-element.33), channel_id=1, source_target_pairs={{0,8},{4,12},{8,16},{12,20},{16,24},{20,28},{24,0},{28,4},{1,9},{5... | collective-permute-start | bytes 786440 | tf_op jit(solution)/shard_map/ppermute | solution.py:201
  24.1 92.8 %collective-permute-start.16 = (f32[8,2,8,1024]{3,2,1,0:T(8,128)}, f32[8,2,8,1024]{3,2,1,0:T(8,128)S(1)}, u32[]{:S(2)}, u32[]{:S(2)}) collective-permute-start(f32[8,2,8,1024]{3,2,1,0:T(8,128)} %get-tuple-element.42), channel_id=1, source_target_pairs={{0,4},{4,8},{8,12},{12,16},{16,20},{20,24},{24,28},{28,0},{1,5},{5... | collective-permute-start | bytes 1572872 | tf_op jit(solution)/shard_map/ppermute | solution.py:201
  25.6 97.3 %collective-permute-start.17 = (f32[8,2,8,1024]{3,2,1,0:T(8,128)}, f32[8,2,8,1024]{3,2,1,0:T(8,128)S(1)}, u32[]{:S(2)}, u32[]{:S(2)}) collective-permute-start(f32[8,2,8,1024]{3,2,1,0:T(8,128)} %get-tuple-element.45), channel_id=1, source_target_pairs={{0,8},{4,12},{8,16},{12,20},{16,24},{20,28},{24,0},{28,4},{1,9},{5... | collective-permute-start | bytes 1572872 | tf_op jit(solution)/shard_map/ppermute | solution.py:201
  27.2 50.8 %collective-permute-start.4 = (f32[8,8,1024]{2,1,0:T(8,128)}, f32[8,8,1024]{2,1,0:T(8,128)S(1)}, u32[]{:S(2)}, u32[]{:S(2)}) collective-permute-start(f32[8,8,1024]{2,1,0:T(8,128)} %get-tuple-element.34), channel_id=1, source_target_pairs={{0,12},{4,16},{8,20},{12,24},{16,28},{20,0},{24,4},{28,8},{1,13},{... | collective-permute-start | bytes 786440 | tf_op jit(solution)/shard_map/ppermute | solution.py:201
  30.3 55.7 %collective-permute-start.5 = (f32[8,8,1024]{2,1,0:T(8,128)}, f32[8,8,1024]{2,1,0:T(8,128)S(1)}, u32[]{:S(2)}, u32[]{:S(2)}) collective-permute-start(f32[8,8,1024]{2,1,0:T(8,128)} %get-tuple-element.35), channel_id=1, source_target_pairs={{0,16},{4,20},{8,24},{12,28},{16,0},{20,4},{24,8},{28,12},{1,17},{... | collective-permute-start | bytes 786440 | tf_op jit(solution)/shard_map/ppermute | solution.py:201
  32.1 59.5 %collective-permute-start.6 = (f32[8,8,1024]{2,1,0:T(8,128)}, f32[8,8,1024]{2,1,0:T(8,128)S(1)}, u32[]{:S(2)}, u32[]{:S(2)}) collective-permute-start(f32[8,8,1024]{2,1,0:T(8,128)} %get-tuple-element.36), channel_id=1, source_target_pairs={{0,20},{4,24},{8,28},{12,0},{16,4},{20,8},{24,12},{28,16},{1,21},{... | collective-permute-start | bytes 786440 | tf_op jit(solution)/shard_map/ppermute | solution.py:201
  78.0 13.7 %collective-permute-start.7 = (f32[8,8,1024]{2,1,0:T(8,128)}, f32[8,8,1024]{2,1,0:T(8,128)S(1)}, u32[]{:S(2)}, u32[]{:S(2)}) collective-permute-start(f32[8,8,1024]{2,1,0:T(8,128)} %get-tuple-element.37), channel_id=1, source_target_pairs={{0,24},{4,28},{8,0},{12,4},{16,8},{20,12},{24,16},{28,20},{1,25},{... | collective-permute-start | bytes 786440 | tf_op jit(solution)/shard_map/ppermute | solution.py:201
  86.0 10.6 %collective-permute-start.8 = (f32[8,8,1024]{2,1,0:T(8,128)}, f32[8,8,1024]{2,1,0:T(8,128)S(1)}, u32[]{:S(2)}, u32[]{:S(2)}) collective-permute-start(f32[8,8,1024]{2,1,0:T(8,128)} %get-tuple-element.38), channel_id=1, source_target_pairs={{0,28},{4,0},{8,4},{12,8},{16,12},{20,16},{24,20},{28,24},{1,29},{... | collective-permute-start | bytes 786440 | tf_op jit(solution)/shard_map/ppermute | solution.py:201
  91.6 31.4 %collective-permute-start.18 = (f32[8,2,8,1024]{3,2,1,0:T(8,128)}, f32[8,2,8,1024]{3,2,1,0:T(8,128)S(1)}, u32[]{:S(2)}, u32[]{:S(2)}) collective-permute-start(f32[8,2,8,1024]{3,2,1,0:T(8,128)} %get-tuple-element.46), channel_id=1, source_target_pairs={{0,12},{4,16},{8,20},{12,24},{16,28},{20,0},{24,4},{28,8},{1,13},{... | collective-permute-start | bytes 1572872 | tf_op jit(solution)/shard_map/ppermute | solution.py:201
  91.7 38.4 %collective-permute-start.19 = (f32[8,2,8,1024]{3,2,1,0:T(8,128)}, f32[8,2,8,1024]{3,2,1,0:T(8,128)S(1)}, u32[]{:S(2)}, u32[]{:S(2)}) collective-permute-start(f32[8,2,8,1024]{3,2,1,0:T(8,128)} %get-tuple-element.47), channel_id=1, source_target_pairs={{0,16},{4,20},{8,24},{12,28},{16,0},{20,4},{24,8},{28,12},{1,17},{... | collective-permute-start | bytes 1572872 | tf_op jit(solution)/shard_map/ppermute | solution.py:201
  96.6 57.4 %collective-permute-start.20 = (f32[8,2,8,1024]{3,2,1,0:T(8,128)}, f32[8,2,8,1024]{3,2,1,0:T(8,128)S(1)}, u32[]{:S(2)}, u32[]{:S(2)}) collective-permute-start(f32[8,2,8,1024]{3,2,1,0:T(8,128)} %get-tuple-element.48), channel_id=1, source_target_pairs={{0,20},{4,24},{8,28},{12,0},{16,4},{20,8},{24,12},{28,16},{1,21},{... | collective-permute-start | bytes 1572872 | tf_op jit(solution)/shard_map/ppermute | solution.py:201
  116.9 41.3 %collective-permute-start.21 = (f32[8,2,8,1024]{3,2,1,0:T(8,128)S(1)}, f32[8,2,8,1024]{3,2,1,0:T(8,128)S(1)}, u32[]{:S(2)}, u32[]{:S(2)}) collective-permute-start(f32[8,2,8,1024]{3,2,1,0:T(8,128)S(1)} %copy-done.7), channel_id=1, source_target_pairs={{0,24},{4,28},{8,0},{12,4},{16,8},{20,12},{24,16},{28,20},{1,25},{... | collective-permute-start | bytes 1572872 | tf_op jit(solution)/shard_map/ppermute | solution.py:201
  122.9 66.3 %collective-permute-start.22 = (f32[8,2,8,1024]{3,2,1,0:T(8,128)S(1)}, f32[8,2,8,1024]{3,2,1,0:T(8,128)S(1)}, u32[]{:S(2)}, u32[]{:S(2)}) collective-permute-start(f32[8,2,8,1024]{3,2,1,0:T(8,128)S(1)} %copy-done.6), channel_id=1, source_target_pairs={{0,28},{4,0},{8,4},{12,8},{16,12},{20,16},{24,20},{28,24},{1,29},{... | collective-permute-start | bytes 1572872 | tf_op jit(solution)/shard_map/ppermute | solution.py:201
  123.0 80.9 %collective-permute-start.9 = (f32[8,1,8,1024]{3,1,2,0:T(1,128)S(1)}, f32[8,1,8,1024]{3,1,2,0:T(1,128)S(1)}, u32[]{:S(2)}, u32[]{:S(2)}) collective-permute-start(f32[8,1,8,1024]{3,1,2,0:T(1,128)S(1)} %bitcast.59), channel_id=1, source_target_pairs={{0,4},{4,8},{8,12},{12,16},{16,20},{20,24},{24,28},{28,0},{1,5},{5... | collective-permute-start | bytes 786440 | tf_op jit(solution)/shard_map/ppermute | solution.py:201
  130.1 78.2 %collective-permute-start.10 = (f32[8,1,8,1024]{3,1,2,0:T(1,128)S(1)}, f32[8,1,8,1024]{3,1,2,0:T(1,128)S(1)}, u32[]{:S(2)}, u32[]{:S(2)}) collective-permute-start(f32[8,1,8,1024]{3,1,2,0:T(1,128)S(1)} %bitcast.58), channel_id=1, source_target_pairs={{0,28},{4,0},{8,4},{12,8},{16,12},{20,16},{24,20},{28,24},{1,29},{... | collective-permute-start | bytes 786440 | tf_op jit(solution)/shard_map/ppermute | solution.py:201
  154.0 62.5 %collective-permute-start.11 = (f32[8,1,8,1024]{3,1,2,0:T(1,128)}, f32[8,1,8,1024]{3,1,2,0:T(1,128)}, u32[]{:S(2)}, u32[]{:S(2)}) collective-permute-start(f32[8,1,8,1024]{3,1,2,0:T(1,128)} %bitcast.15), channel_id=1, source_target_pairs={{0,24},{4,28},{8,0},{12,4},{16,8},{20,12},{24,16},{28,20},{1,25},{... | collective-permute-start | bytes 786440 | tf_op jit(solution)/shard_map/ppermute | solution.py:201
  158.2 67.3 %collective-permute-start.12 = (f32[8,1,8,1024]{3,1,2,0:T(1,128)}, f32[8,1,8,1024]{3,1,2,0:T(1,128)}, u32[]{:S(2)}, u32[]{:S(2)}) collective-permute-start(f32[8,1,8,1024]{3,1,2,0:T(1,128)} %bitcast.16), channel_id=1, source_target_pairs={{0,8},{4,12},{8,16},{12,20},{16,24},{20,28},{24,0},{28,4},{1,9},{5... | collective-permute-start | bytes 786440 | tf_op jit(solution)/shard_map/ppermute | solution.py:201
  189.2 43.3 %collective-permute-start.13 = (f32[8,1,8,1024]{3,1,2,0:T(1,128)}, f32[8,1,8,1024]{3,1,2,0:T(1,128)S(1)}, u32[]{:S(2)}, u32[]{:S(2)}) collective-permute-start(f32[8,1,8,1024]{3,1,2,0:T(1,128)} %bitcast.17), channel_id=1, source_target_pairs={{0,20},{4,24},{8,28},{12,0},{16,4},{20,8},{24,12},{28,16},{1,21},{... | collective-permute-start | bytes 786440 | tf_op jit(solution)/shard_map/ppermute | solution.py:201
  204.0 33.4 %collective-permute-start.14 = (f32[8,1,8,1024]{3,1,2,0:T(1,128)}, f32[8,1,8,1024]{3,1,2,0:T(1,128)}, u32[]{:S(2)}, u32[]{:S(2)}) collective-permute-start(f32[8,1,8,1024]{3,1,2,0:T(1,128)} %bitcast.18), channel_id=1, source_target_pairs={{0,12},{4,16},{8,20},{12,24},{16,28},{20,0},{24,4},{28,8},{1,13},{... | collective-permute-start | bytes 786440 | tf_op jit(solution)/shard_map/ppermute | solution.py:201
  208.2 30.8 %collective-permute-start.15 = (f32[8,1,8,1024]{3,1,2,0:T(1,128)}, f32[8,1,8,1024]{3,1,2,0:T(1,128)}, u32[]{:S(2)}, u32[]{:S(2)}) collective-permute-start(f32[8,1,8,1024]{3,1,2,0:T(1,128)} %bitcast.19), channel_id=1, source_target_pairs={{0,16},{4,20},{8,24},{12,28},{16,0},{20,4},{24,8},{28,12},{1,17},{... | collective-permute-start | bytes 786440 | tf_op jit(solution)/shard_map/ppermute | solution.py:201
  216.5 28.2 %collective-permute-start.23 = (f32[8,2,8,1024]{3,2,1,0:T(8,128)}, f32[8,2,8,1024]{3,2,1,0:T(8,128)}, u32[]{:S(2)}, u32[]{:S(2)}) collective-permute-start(f32[8,2,8,1024]{3,2,1,0:T(8,128)} %slice.135), channel_id=1, source_target_pairs={{0,4},{4,8},{8,12},{12,16},{16,20},{20,24},{24,28},{28,0},{1,5},{5... | collective-permute-start | bytes 1572872 | tf_op jit(solution)/shard_map/ppermute | solution.py:201
  225.5 29.1 %collective-permute-start.24 = (f32[8,2,8,1024]{3,2,1,0:T(8,128)}, f32[8,2,8,1024]{3,2,1,0:T(8,128)}, u32[]{:S(2)}, u32[]{:S(2)}) collective-permute-start(f32[8,2,8,1024]{3,2,1,0:T(8,128)} %slice.137), channel_id=1, source_target_pairs={{0,28},{4,0},{8,4},{12,8},{16,12},{20,16},{24,20},{28,24},{1,29},{... | collective-permute-start | bytes 1572872 | tf_op jit(solution)/shard_map/ppermute | solution.py:201
  232.5 27.8 %collective-permute-start.25 = (f32[8,2,8,1024]{3,2,1,0:T(8,128)}, f32[8,2,8,1024]{3,2,1,0:T(8,128)}, u32[]{:S(2)}, u32[]{:S(2)}) collective-permute-start(f32[8,2,8,1024]{3,2,1,0:T(8,128)} %slice.139), channel_id=1, source_target_pairs={{0,24},{4,28},{8,0},{12,4},{16,8},{20,12},{24,16},{28,20},{1,25},{... | collective-permute-start | bytes 1572872 | tf_op jit(solution)/shard_map/ppermute | solution.py:201
  233.9 19.8 %copy-start = (f32[8,2,8,1024]{3,2,1,0:T(8,128)S(1)}, f32[8,2,8,1024]{3,2,1,0:T(8,128)}, u32[]{:S(2)}) copy-start(f32[8,2,8,1024]{3,2,1,0:T(8,128)} %slice.133) | copy-start | bytes 1572868
  237.4 28.6 %collective-permute-start.26 = (f32[8,2,8,1024]{3,2,1,0:T(8,128)}, f32[8,2,8,1024]{3,2,1,0:T(8,128)}, u32[]{:S(2)}, u32[]{:S(2)}) collective-permute-start(f32[8,2,8,1024]{3,2,1,0:T(8,128)} %slice.141), channel_id=1, source_target_pairs={{0,8},{4,12},{8,16},{12,20},{16,24},{20,28},{24,0},{28,4},{1,9},{5... | collective-permute-start | bytes 1572872 | tf_op jit(solution)/shard_map/ppermute | solution.py:201
  239.1 38.0 %collective-permute-start.27 = (f32[8,2,8,1024]{3,2,1,0:T(8,128)S(1)}, f32[8,2,8,1024]{3,2,1,0:T(8,128)}, u32[]{:S(2)}, u32[]{:S(2)}) collective-permute-start(f32[8,2,8,1024]{3,2,1,0:T(8,128)S(1)} %slice.143), channel_id=1, source_target_pairs={{0,20},{4,24},{8,28},{12,0},{16,4},{20,8},{24,12},{28,16},{1,21},{... | collective-permute-start | bytes 1572872 | tf_op jit(solution)/shard_map/ppermute | solution.py:201
  244.7 65.5 %collective-permute-start.28 = (f32[8,2,8,1024]{3,2,1,0:T(8,128)S(1)}, f32[8,2,8,1024]{3,2,1,0:T(8,128)S(1)}, u32[]{:S(2)}, u32[]{:S(2)}) collective-permute-start(f32[8,2,8,1024]{3,2,1,0:T(8,128)S(1)} %slice.145), channel_id=1, source_target_pairs={{0,12},{4,16},{8,20},{12,24},{16,28},{20,0},{24,4},{28,8},{1,13},{... | collective-permute-start | bytes 1572872 | tf_op jit(solution)/shard_map/ppermute | solution.py:201
  254.6 67.0 %collective-permute-start.29 = (f32[8,2,8,1024]{3,2,1,0:T(8,128)S(1)}, f32[8,2,8,1024]{3,2,1,0:T(8,128)S(1)}, u32[]{:S(2)}, u32[]{:S(2)}) collective-permute-start(f32[8,2,8,1024]{3,2,1,0:T(8,128)S(1)} %slice.147), channel_id=1, source_target_pairs={{0,16},{4,20},{8,24},{12,28},{16,0},{20,4},{24,8},{28,12},{1,17},{... | collective-permute-start | bytes 1572872 | tf_op jit(solution)/shard_map/ppermute | solution.py:201
  (7 other events, 49.5 us)
